TPU v7x, 32 devices: a whole 2x2x4 slice. The times are simulated.
32 devices in a mesh: seq: 2 (over core), mp: 4 (over y, x), batch: 4 (over z).
Axes of the slice: x: 2, y: 2, z: 4, core: 2. Of those that a mesh axis runs over, the one named last changes fastest.
Arguments:
- queries: bfloat16 [4, 8, 4096], P('batch', 'seq', 'mp'), may hold values from -6 to 6
- keys: bfloat16 [4, 512, 1024], P('batch', 'seq', 'mp'), may hold values from -6 to 6
- values: bfloat16 [4, 512, 1024], P('batch', 'seq', 'mp'), may hold values from -6 to 6
- key_position: float32 [32, 128], replicated, may hold values from -4 to 4
- compress_keys: bfloat16 [4096, 128], replicated, may hold values from -0.2 to 0.2
- compress_values: bfloat16 [4096, 128], replicated, may hold values from -0.09375 to 0.09375
- out_proj: bfloat16 [4096, 4096], P('mp', 'seq'), may hold values from -0.09375 to 0.09375
- residual: bfloat16 [4, 8, 4096], P(None, None, 'seq'), may hold values from -6 to 6
- norm_gain: float32 [4096], replicated, may hold values from 0.25 to 1.75
- lm_head: bfloat16 [8192, 4096], P(('seq', 'mp', 'batch')), may hold values from -0.4 to 0.4
- targets: int32 [4, 8], replicated, may hold values from 0 to 8191
- lengths: int32 [4], replicated, may hold values from 128 to 512
Outputs:
- token_logprob: float32 [4, 8], P('batch', 'seq')
- rollout_score: float32 [4], P('batch')
All inputs are finite; a program needn't handle non-finite values.
Results may differ from a plain program's by a relative error of at most 0.0005.
The roundings to bfloat16 on the way count: a program that leaves them out, or rounds other values in their place, can miss the bound.
Values may be sent and summed in bfloat16 or wider, within the bound.
No kernel may reach another device: no remote copies, remote signals or barrier semaphores. Data moves between devices by JAX's collectives and lax.ppermute only.
A program may use at most 64 MiB of HBM per device.

v0:
```python
import math

import jax
import jax.numpy as jnp
from jax import lax
from jax.sharding import PartitionSpec as P

HEAD_DIM = 128
BLOCK = 32
STRIDE = 16


def from_behind(block, axis, distance):
    devices = range(lax.axis_size(axis))
    route = [(i - distance, i) for i in devices if i - distance in devices]
    return lax.ppermute(block, axis, route)


def compress_rows(rows, following, position, weight):
    extended = jnp.concatenate([rows, following], 0)
    count = rows.shape[0] // STRIDE
    heads = rows.shape[1] // HEAD_DIM
    shaped = extended.reshape(count + 1, STRIDE, heads, HEAD_DIM)
    blocks = jnp.concatenate([shaped[:-1], shaped[1:]], 1)
    blocks = (blocks.astype(jnp.float32) + position[None, :, None, :]).astype(jnp.bfloat16)
    mapped = jnp.einsum(
        "bjhd,jde->bhe",
        blocks,
        weight.reshape(BLOCK, HEAD_DIM, HEAD_DIM),
        preferred_element_type=jnp.float32,
    )
    return mapped.astype(jnp.bfloat16).reshape(count, heads * HEAD_DIM)


def normalize(hidden, gain):
    widened = hidden.astype(jnp.float32)
    meansq = jnp.mean(widened * widened, -1, keepdims=True)
    return (widened * lax.rsqrt(meansq + 1e-05) * gain).astype(jnp.bfloat16)


def vocab_logits(normed, rows):
    return lax.dot_general(
        normed, rows, (((1,), (1,)), ((), ())), preferred_element_type=jnp.float32
    )


def picked_logit(logits, offset, wanted):
    columns = offset + jnp.arange(logits.shape[1], dtype=jnp.int32)
    hits = columns[None, :] == wanted[:, None]
    return jnp.sum(jnp.where(hits, logits, 0.0), 1)


def body(
    queries,
    keys,
    values,
    key_position,
    compress_keys,
    compress_values,
    out_proj,
    residual,
    norm_gain,
    lm_head,
    targets,
    lengths,
):
    seq_count = lax.axis_size("seq")
    seq_pos = lax.axis_index("seq")
    batch_count = lax.axis_size("batch")
    batch_pos = lax.axis_index("batch")
    qcount = queries.shape[1]
    skip = keys.shape[1] // qcount
    scored = targets.shape[1]
    following = from_behind((keys[0, :STRIDE], values[0, :STRIDE]), "seq", -1)
    comp_keys = compress_rows(keys[0], following[0], key_position, compress_keys)
    comp_values = compress_rows(values[0], following[1], key_position, compress_values)
    every = lax.all_gather(jnp.stack([comp_keys, comp_values], 0), "seq", axis=1, tiled=True)
    heads = keys.shape[2] // HEAD_DIM
    blocks = every.shape[1]
    all_keys = every[0].reshape(blocks, heads, HEAD_DIM)
    all_values = every[1].reshape(blocks, heads, HEAD_DIM)
    group = queries.shape[2] // HEAD_DIM // heads
    query = queries[0].reshape(qcount, heads, group, HEAD_DIM)
    scores = jnp.einsum("qhgd,bhd->qhgb", query, all_keys, preferred_element_type=jnp.float32) * (
        1.0 / math.sqrt(HEAD_DIM)
    )
    index = seq_pos * qcount + jnp.arange(qcount, dtype=jnp.int32)
    limit = index * skip // STRIDE
    visible = (jnp.arange(blocks, dtype=jnp.int32)[None, :] <= limit[:, None])[:, None, None, :]
    scores = jnp.where(visible, scores, -1e30)
    peak = jnp.max(scores, -1, keepdims=True)
    weights = jnp.where(visible, jnp.exp(scores - peak), 0.0)
    probs = (weights / jnp.sum(weights, -1, keepdims=True)).astype(jnp.bfloat16)
    attended = jnp.einsum("qhgb,bhd->qhgd", probs, all_values, preferred_element_type=jnp.float32)
    attended = attended.astype(jnp.bfloat16).reshape(qcount, heads * group * HEAD_DIM)
    spots = jnp.arange(scored, dtype=jnp.int32) * skip + BLOCK - 1
    valid = (spots[None, :] < lengths[:, None]).astype(jnp.float32)
    count = jnp.sum(valid)
    width = out_proj.shape[1]
    rows_all = lax.all_gather(attended, ("seq", "batch"), axis=0, tiled=True)
    part = jnp.dot(rows_all, out_proj, preferred_element_type=jnp.float32)
    summed = lax.psum(part, "mp")
    local_res = (
        residual.reshape(batch_count, seq_count, qcount, width)
        .transpose(1, 0, 2, 3)
        .reshape(-1, width)
    )
    hidden = (local_res.astype(jnp.float32) + summed).astype(jnp.bfloat16)
    whole = lax.all_gather(hidden, "seq", axis=1, tiled=True)
    normed = normalize(whole, norm_gain)
    logits = vocab_logits(normed, lm_head)
    wanted = targets.reshape(batch_count, seq_count, qcount).transpose(1, 0, 2).reshape(-1)
    offset = lax.axis_index(("seq", "mp", "batch")) * lm_head.shape[0]
    picked = picked_logit(logits, offset, wanted)
    local_top = jnp.max(logits, 1)
    top = lax.pmax(local_top, ("seq", "mp", "batch"))
    local_sum = jnp.sum(jnp.exp(logits - top[:, None]), 1)
    total, target_logit = lax.psum((local_sum, picked), ("seq", "mp", "batch"))
    logprob = target_logit - (top + jnp.log(total))
    cube = logprob.reshape(seq_count, batch_count, qcount)
    token_logprob = cube[seq_pos, batch_pos][None, :]
    by_rollout = cube.transpose(1, 0, 2).reshape(batch_count, scored)
    sums = jnp.sum(valid * by_rollout, 1) / count
    rollout_score = sums[batch_pos][None]
    return (token_logprob, rollout_score)


def solution(mesh):
    in_specs = (
        P("batch", "seq", "mp"),
        P("batch", "seq", "mp"),
        P("batch", "seq", "mp"),
        P(),
        P(),
        P(),
        P("mp", "seq"),
        P(None, None, "seq"),
        P(),
        P(("seq", "mp", "batch"), None),
        P(),
        P(),
    )
    out_specs = (P("batch", "seq"), P("batch"))
    return jax.shard_map(body, mesh=mesh, in_specs=in_specs, out_specs=out_specs, check_vma=False)
```

profile of v0, /device:TPU:0, one launch (start us, length us, event | category | flops | bytes accessed | tf_op | source)
XLA Modules:
  0.0 194.4 jit_solution(1485913314387452292)
XLA Ops:
  7.2 0.0 copy-start
  7.2 0.0 copy-start.1
  7.2 0.0 all-reduce.3.cloned.1.call-start
  7.2 0.9 slice_bitcast_fusion.1
  8.1 1.4 collective-permute-start
  9.5 1.3 slice_bitcast_fusion
  10.8 1.3 collective-permute-start.1
  12.1 0.6 iota_compare_fusion
  12.7 0.6 multiply_add_fusion
  13.3 0.9 slice.32
  14.3 0.9 slice.36
  15.2 0.7 copy.47
  15.9 0.1 copy.50
  16.0 1.3 reshape_squeeze.11
  17.3 0.0 collective-permute-done
  17.3 0.9 pad_maximum_fusion.1
  18.2 0.1 copy.48
  18.3 1.6 fusion.6
  19.9 0.0 collective-permute-done.1
  19.9 0.9 pad_maximum_fusion
  20.9 0.0 copy-start.2
  20.9 0.1 copy.51
  21.0 0.0 copy-done.1
  21.0 0.0 copy-start.4
  21.0 0.0 copy-start.6
  21.0 1.0 fusion.7
  22.0 0.0 copy-start.3
  22.1 2.6 %all_gather.9 = bf16[2,32,256]{2,1,0:T(8,128)(2,1)S(1)} all-gather(bf16[2,16,256]{2,1,0:T(8,128)(2,1)S(1)} %pad_maximum_fusion.2), channel_id=1, replica_groups=mesh['seq'=2,'mp'=4,'batch'=4] {'seq'}, dimensions={1}, use_global_device_ids=true | all-gather | bytes 49152 | tf_op jit(solution)/shard_map/all_gather | solution.py:77
  24.7 0.8 fusion.5
  25.5 0.8 fusion.32
  26.4 0.9 fusion.8
  27.3 25.7 %all-gather = bf16[8,4,1024]{2,1,0:T(4,128)(2,1)S(1)} all-gather(bf16[1,4,1024]{2,1,0:T(4,128)(2,1)S(1)} %reshape.113), channel_id=1, replica_groups=mesh['seq'=2,'mp'=4,'batch'=4] {'seq','batch'}, dimensions={0}, use_global_device_ids=true | all-gather | bytes 73728 | tf_op jit(solution)/shard_map/all_gather | solution.py:100
  53.0 0.0 copy-start.5
  53.0 3.7 %fusion.34 = f32[32,2048]{1,0:T(8,128)} fusion(bf16[32,1024]{1,0:T(8,128)(2,1)S(1)} %reshape.114, bf16[1024,2048]{1,0:T(8,128)(2,1)} %param.18), kind=kOutput, calls=%fused_computation.65 | convolution fusion | flops 134217728 | bytes 4521984 | tf_op jit(solution)/shard_map/dot_general | solution.py:101
  56.7 0.0 all-reduce.3.cloned.1.call-update
  56.8 0.0 copy-done.2
  56.8 0.1 reshape.112
  56.9 0.1 reshape.111
  57.0 0.0 copy-done.4
  57.0 0.1 reshape.106
  57.1 0.1 eq.16
  57.2 0.0 copy-done.6
  57.2 0.7 convert_reduce_fusion
  57.9 43.1 %all-reduce.3.cloned.1.call-done = f32[32,2048]{1,0:T(8,128)} async-done(((f32[32,2048]{1,0:T(8,128)}), f32[32,2048]{1,0:T(8,128)}) %all-reduce.3.cloned.1.call-update) | async-done | bytes 262160 | tf_op jit(solution)/shard_map/psum | solution.py:102
  101.0 1.0 add_convert_fusion.4
  102.0 2.0 %all_gather.11 = bf16[32,4096]{1,0:T(8,128)(2,1)S(1)} all-gather(bf16[32,2048]{1,0:T(8,128)(2,1)S(1)} %add_convert_fusion.4), channel_id=1, replica_groups=mesh['seq'=2,'mp'=4,'batch'=4] {'seq'}, dimensions={1}, use_global_device_ids=true | all-gather | bytes 393216 | tf_op jit(solution)/shard_map/all_gather | solution.py:109
  104.0 0.2 fusion.9
  104.1 0.0 copy-done
  104.1 0.0 copy-done.3
  104.2 0.8 fusion.33
  105.0 39.3 %pmax.7 = f32[32]{0:T(128)S(1)} all-reduce(f32[32]{0:T(128)S(1)} %get-tuple-element.8), channel_id=1, replica_groups=mesh['seq'=2,'mp'=4,'batch'=4] {'seq','mp','batch'}, use_global_device_ids=true, to_apply=%region_7.8 | all-reduce | flops 32 | bytes 256 | tf_op jit(solution)/shard_map/pmax | solution.py:116
  144.3 0.2 exponential_reduce_fusion
  144.5 41.0 %all-reduce = (f32[32]{0:T(128)S(1)}, f32[32]{0:T(128)S(1)}) all-reduce(f32[32]{0:T(128)S(1)} %get-tuple-element.3, f32[32]{0:T(128)S(1)} %get-tuple-element.2), channel_id=1, replica_groups=mesh['seq'=2,'mp'=4,'batch'=4] {'seq','mp','batch'}, use_global_device_ids=true, to_apply=%region_5.6 | all-reduce | flops 64 | bytes 512 | tf_op jit(solution)/shard_map/psum | solution.py:118
  185.5 0.1 reshape.110
  185.6 0.0 copy-done.5
  185.6 0.2 fusion.28
  185.8 0.7 broadcast_divide_fusion
  186.4 0.6 dynamic_slice.7
  187.0 0.5 dynamic-slice_bitcast_fusion
  (20 shorter events, 0.2 us)
Async XLA Ops:
  7.2 97.0 %copy-start = (bf16[256,4096]{1,0:T(8,128)(2,1)S(1)}, bf16[256,4096]{1,0:T(8,128)(2,1)}, u32[]{:S(2)}) copy-start(bf16[256,4096]{1,0:T(8,128)(2,1)} %param.21) | copy-start | bytes 6291460
  7.2 13.8 %copy-start.1 = (bf16[4096,128]{1,0:T(8,128)(2,1)S(1)}, bf16[4096,128]{1,0:T(8,128)(2,1)}, u32[]{:S(2)}) copy-start(bf16[4096,128]{1,0:T(8,128)(2,1)} %param.17) | copy-start | bytes 3145732
  7.2 93.8 %all-reduce.3.cloned.1.call-start = ((), (), s32[]{:S(2)}) async-start(), calls=%async_computation | async-start | bytes 524288 | tf_op jit(solution)/shard_map/psum | solution.py:102
  8.1 9.1 %collective-permute-start = (bf16[16,256]{1,0:T(8,128)(2,1)S(1)}, bf16[16,256]{1,0:T(8,128)(2,1)S(1)}, u32[]{:S(2)}, u32[]{:S(2)}) collective-permute-start(bf16[16,256]{1,0:T(8,128)(2,1)S(1)} %slice_bitcast_fusion.1), channel_id=1, source_target_pairs={{16,0},{17,1},{18,2},{19,3},{20,4},{21,5},{22,6},{23,7},{24,8},{25... | collective-permute-start | bytes 24584 | tf_op jit(solution)/shard_map/ppermute | solution.py:16
  10.8 9.1 %collective-permute-start.1 = (bf16[16,256]{1,0:T(8,128)(2,1)}, bf16[16,256]{1,0:T(8,128)(2,1)S(1)}, u32[]{:S(2)}, u32[]{:S(2)}) collective-permute-start(bf16[16,256]{1,0:T(8,128)(2,1)} %slice_bitcast_fusion), channel_id=1, source_target_pairs={{16,0},{17,1},{18,2},{19,3},{20,4},{21,5},{22,6},{23,7},{24,8},{25... | collective-permute-start | bytes 24584 | tf_op jit(solution)/shard_map/ppermute | solution.py:16
  20.9 35.9 %copy-start.2 = (bf16[4,8,2048]{2,1,0:T(8,128)(2,1)S(1)}, bf16[4,8,2048]{2,1,0:T(8,128)(2,1)}, u32[]{:S(2)}) copy-start(bf16[4,8,2048]{2,1,0:T(8,128)(2,1)} %param.19) | copy-start | bytes 393220
  21.0 36.0 %copy-start.4 = (s32[4,8]{1,0:T(4,128)S(1)}, s32[4,8]{1,0:T(4,128)}, u32[]{:S(2)}) copy-start(s32[4,8]{1,0:T(4,128)} %param.22) | copy-start | bytes 388
  21.0 36.2 %copy-start.6 = (s32[4]{0:T(128)S(1)}, s32[4]{0:T(128)}, u32[]{:S(2)}) copy-start(s32[4]{0:T(128)} %param.23) | copy-start | bytes 52
  22.0 82.1 %copy-start.3 = (f32[4096]{0:T(1024)S(1)}, f32[4096]{0:T(1024)}, u32[]{:S(2)}) copy-start(f32[4096]{0:T(1024)} %param.20) | copy-start | bytes 49156
  53.0 132.6 %copy-start.5 = (s32[2,4]{1,0:T(2,128)S(1)}, s32[2,4]{1,0:T(2,128)}, u32[]{:S(2)}) copy-start(s32[2,4]{1,0:T(2,128)} %multiply_add_fusion) | copy-start | bytes 100
Sparse Core Ops, SparseCore 0:
  56.9 44.0 all-reduce.2
where the time goes:
time: 195 us; the launch traced here: 194 us
  blocking collectives  111 us (57%)
  waiting for transfers between devices  43.1 us (22%)
  between operations  14.3 us (7%)
  matrix products  8.86 us (5%)
  local copies, waits for them, and re-layouts  8.01 us (4%)
  other arithmetic  6.72 us (3%)
  starting transfers between devices  2.73 us (1%)
    psum x1, waiting for transfers between devices, body(): summed = lax.psum(part, 'mp')  43.1 us
    psum x1, blocking collectives, body(): total, target_logit = lax.psum((local_sum, picked), ('seq', 'mp', 'batch'))  41 us
    pmax x1, blocking collectives, body(): top = lax.pmax(local_top, ('seq', 'mp', 'batch'))  39.3 us
    all_gather x1, blocking collectives, body(): rows_all = lax.all_gather(attended, ('seq', 'batch'), axis=0, tiled=True)  25.7 us
  transfers between devices with their start and end apart: 3, of which 1 were waited for; matrix products, arithmetic and copies ran while one was open for 5% of the time, Pallas kernels for 0%

commit v1 on v0

v1 whole, which is shorter than its diff:
```python
import math

import jax
import jax.numpy as jnp
from jax import lax
from jax.sharding import PartitionSpec as P

HEAD_DIM = 128
BLOCK = 32
STRIDE = 16


def from_behind(block, axis, distance):
    devices = range(lax.axis_size(axis))
    route = [(i - distance, i) for i in devices if i - distance in devices]
    return lax.ppermute(block, axis, route)


def compress_rows(rows, following, position, weight):
    extended = jnp.concatenate([rows, following], 0)
    count = rows.shape[0] // STRIDE
    heads = rows.shape[1] // HEAD_DIM
    shaped = extended.reshape(count + 1, STRIDE, heads, HEAD_DIM)
    blocks = jnp.concatenate([shaped[:-1], shaped[1:]], 1)
    blocks = (blocks.astype(jnp.float32) + position[None, :, None, :]).astype(jnp.bfloat16)
    mapped = jnp.einsum(
        "bjhd,jde->bhe",
        blocks,
        weight.reshape(BLOCK, HEAD_DIM, HEAD_DIM),
        preferred_element_type=jnp.float32,
    )
    return mapped.astype(jnp.bfloat16).reshape(count, heads * HEAD_DIM)


def normalize(hidden, gain):
    widened = hidden.astype(jnp.float32)
    meansq = jnp.mean(widened * widened, -1, keepdims=True)
    return (widened * lax.rsqrt(meansq + 1e-05) * gain).astype(jnp.bfloat16)


def vocab_logits(normed, rows):
    return lax.dot_general(
        normed, rows, (((1,), (1,)), ((), ())), preferred_element_type=jnp.float32
    )


def picked_logit(logits, offset, wanted):
    columns = offset + jnp.arange(logits.shape[1], dtype=jnp.int32)
    hits = columns[None, :] == wanted[:, None]
    return jnp.sum(jnp.where(hits, logits, 0.0), 1)

DIRECT = 4
SPREAD = 64


def pairs(axis, distance):
    return [(i, i ^ distance) for i in range(lax.axis_size(axis))]


def direct(axis):
    count = lax.axis_size(axis)
    return count <= DIRECT and count & (count - 1) == 0


def exchange(block, axis):
    return [block] + [
        lax.ppermute(block, axis, pairs(axis, distance))
        for distance in range(1, lax.axis_size(axis))
    ]


def by_position(blocks, axis):
    place = lax.axis_index(axis)
    step = 1
    while step < len(blocks):
        odd = (place // step) % 2 == 1
        blocks = [jnp.where(odd, blocks[i ^ step], blocks[i]) for i in range(len(blocks))]
        step *= 2
    return blocks


def pair_sum(blocks):
    while len(blocks) > 1:
        blocks = [blocks[i] + blocks[i + 1] for i in range(0, len(blocks), 2)]
    return blocks[0]


def sum_over(part, axis):
    if direct(axis):
        return pair_sum(exchange(part, axis))
    return lax.psum(part, axis)


def gather_over(block, axis, dimension):
    if direct(axis):
        return jnp.concatenate(by_position(exchange(block, axis), axis), dimension)
    return lax.all_gather(block, axis, axis=dimension, tiled=True)


def attend(query, all_keys, all_values, first, skip):
    count = query.shape[0]
    blocks = all_keys.shape[0]
    scores = jnp.einsum("qhgd,bhd->qhgb", query, all_keys, preferred_element_type=jnp.float32) * (
        1.0 / math.sqrt(HEAD_DIM)
    )
    index = first + jnp.arange(count, dtype=jnp.int32)
    limit = index * skip // STRIDE
    visible = (jnp.arange(blocks, dtype=jnp.int32)[None, :] <= limit[:, None])[:, None, None, :]
    scores = jnp.where(visible, scores, -1e30)
    peak = jnp.max(scores, -1, keepdims=True)
    weights = jnp.where(visible, jnp.exp(scores - peak), 0.0)
    probs = (weights / jnp.sum(weights, -1, keepdims=True)).astype(jnp.bfloat16)
    attended = jnp.einsum("qhgb,bhd->qhgd", probs, all_values, preferred_element_type=jnp.float32)
    return attended.astype(jnp.bfloat16).reshape(count, -1)


def attend_whole(queries, keys, values, key_position, compress_keys, compress_values, skip):
    rows = gather_over(keys, "seq", 0)
    vals = gather_over(values, "seq", 0)
    query = gather_over(queries, "seq", 0)
    none = jnp.zeros((STRIDE, rows.shape[1]), rows.dtype)
    comp_keys = compress_rows(rows, none, key_position, compress_keys)
    comp_values = compress_rows(vals, none, key_position, compress_values)
    heads = rows.shape[1] // HEAD_DIM
    group = query.shape[1] // HEAD_DIM // heads
    return attend(
        query.reshape(-1, heads, group, HEAD_DIM),
        comp_keys.reshape(-1, heads, HEAD_DIM),
        comp_values.reshape(-1, heads, HEAD_DIM),
        0,
        skip,
    )


def attend_segments(queries, keys, values, key_position, compress_keys, compress_values, skip):
    following = from_behind((keys[:STRIDE], values[:STRIDE]), "seq", -1)
    comp_keys = compress_rows(keys, following[0], key_position, compress_keys)
    comp_values = compress_rows(values, following[1], key_position, compress_values)
    every = lax.all_gather(jnp.stack([comp_keys, comp_values], 0), "seq", axis=1, tiled=True)
    heads = keys.shape[1] // HEAD_DIM
    group = queries.shape[1] // HEAD_DIM // heads
    blocks = every.shape[1]
    attended = attend(
        queries.reshape(-1, heads, group, HEAD_DIM),
        every[0].reshape(blocks, heads, HEAD_DIM),
        every[1].reshape(blocks, heads, HEAD_DIM),
        lax.axis_index("seq") * queries.shape[0],
        skip,
    )
    return lax.all_gather(attended, "seq", axis=0, tiled=True)


EVERY = ("seq", "mp", "batch")


def log_probs(logits, wanted, offset):
    picked = picked_logit(logits, offset, wanted)
    local_top = jnp.max(logits, 1)
    devices = lax.axis_size(EVERY)
    if devices > SPREAD:
        top = lax.pmax(local_top, EVERY)
        local_sum = jnp.sum(jnp.exp(logits - top[:, None]), 1)
        total, target_logit = lax.psum((local_sum, picked), EVERY)
        return target_logit - (top + jnp.log(total))
    local_sum = jnp.sum(jnp.exp(logits - local_top[:, None]), 1)
    mine = jnp.concatenate([local_top, local_sum, picked], 0)
    sent = jnp.broadcast_to(mine[None, :], (devices, mine.shape[0]))
    tops, sums, hits = jnp.split(lax.all_to_all(sent, EVERY, 0, 0, tiled=True), 3, 1)
    top = jnp.max(tops, 0)
    total = jnp.sum(sums * jnp.exp(tops - top[None, :]), 0)
    return jnp.sum(hits, 0) - (top + jnp.log(total))


def body(
    queries,
    keys,
    values,
    key_position,
    compress_keys,
    compress_values,
    out_proj,
    residual,
    norm_gain,
    lm_head,
    targets,
    lengths,
):
    seq_pos = lax.axis_index("seq")
    batch_pos = lax.axis_index("batch")
    qcount = queries.shape[1]
    skip = keys.shape[1] // qcount
    rollouts, scored = targets.shape
    attention = attend_whole if direct("seq") else attend_segments
    attended = attention(
        queries[0], keys[0], values[0], key_position, compress_keys, compress_values, skip
    )
    part = jnp.dot(attended, out_proj, preferred_element_type=jnp.float32)
    summed = sum_over(part, "mp")
    hidden = (residual[batch_pos].astype(jnp.float32) + summed).astype(jnp.bfloat16)
    whole = gather_over(gather_over(hidden, "batch", 0), "seq", 1)
    normed = normalize(whole, norm_gain)
    logits = vocab_logits(normed, lm_head)
    offset = lax.axis_index(EVERY) * lm_head.shape[0]
    by_rollout = log_probs(logits, targets.reshape(-1), offset).reshape(rollouts, scored)
    spots = jnp.arange(scored, dtype=jnp.int32) * skip + BLOCK - 1
    valid = (spots[None, :] < lengths[:, None]).astype(jnp.float32)
    count = jnp.sum(valid)
    token_logprob = lax.dynamic_slice(by_rollout, (batch_pos, seq_pos * qcount), (1, qcount))
    sums = jnp.sum(valid * by_rollout, 1) / count
    rollout_score = sums[batch_pos][None]
    return (token_logprob, rollout_score)


def solution(mesh):
    in_specs = (
        P("batch", "seq", "mp"),
        P("batch", "seq", "mp"),
        P("batch", "seq", "mp"),
        P(),
        P(),
        P(),
        P("mp", "seq"),
        P(None, None, "seq"),
        P(),
        P(("seq", "mp", "batch"), None),
        P(),
        P(),
    )
    out_specs = (P("batch", "seq"), P("batch"))
    return jax.shard_map(body, mesh=mesh, in_specs=in_specs, out_specs=out_specs, check_vma=False)
```

time: 195 us -> 47 us (0.24)
  blocking collectives: 111 us -> 0 us
  waiting for transfers between devices: 43.1 us -> 18.5 us
  between operations: 14.3 us -> 0.87 us
  starting transfers between devices: 2.73 us -> 12.5 us
  local copies, waits for them, and re-layouts: 8.01 us -> 2.75 us
    psum x1 -> x0, waiting for transfers between devices: 43.1 us -> none  [body(): summed = lax.psum(part, 'mp')]
    psum x1 -> x0, blocking collectives: 41 us -> none  [body(): total, target_logit = lax.psum((local_sum, picked), ('seq', 'mp', 'batch'))]
    pmax x1 -> x0, blocking collectives: 39.3 us -> none  [body(): top = lax.pmax(local_top, ('seq', 'mp', 'batch'))]
    all_gather x3 -> x0, blocking collectives: 30.3 us -> none  [the longest x1 25.7 us: body(): rows_all = lax.all_gather(attended, ('seq', 'batch'), axis=0, tiled=True)]
    ppermute x2 -> x10, waiting for transfers between devices: 0.01 us -> 11.3 us  [exchange(): lax.ppermute(block, axis, pairs(axis, distance))]
    ppermute x2 -> x10, starting transfers between devices: 2.69 us -> 9.91 us  [exchange(): lax.ppermute(block, axis, pairs(axis, distance))]
    all_to_all x0 -> x1, waiting for transfers between devices: none -> 7.14 us  [log_probs(): lax.all_to_all(sent, EVERY, 0, 0, tiled=True)]
    all_to_all x0 -> x1, starting transfers between devices: none -> 2.57 us  [log_probs(): lax.all_to_all(sent, EVERY, 0, 0, tiled=True)]
  transfers between devices with their start and end apart: 3 -> 11, of which waited for: 1 -> 8; matrix products, arithmetic and copies ran while one was open for 5% -> 2% of each run, Pallas kernels for 0% -> 0%
where the time goes in v1:
time: 47 us; the launch traced here: 46.7 us
  waiting for transfers between devices  18.5 us (39%)
  starting transfers between devices  12.5 us (27%)
  matrix products  7.05 us (15%)
  other arithmetic  5.06 us (11%)
  local copies, waits for them, and re-layouts  2.75 us (6%)
  between operations  0.87 us (2%)
    ppermute x10, waiting for transfers between devices, exchange(): lax.ppermute(block, axis, pairs(axis, distance))  11.3 us
    ppermute x10, starting transfers between devices, exchange(): lax.ppermute(block, axis, pairs(axis, distance))  9.91 us
    all_to_all x1, waiting for transfers between devices, log_probs(): lax.all_to_all(sent, EVERY, 0, 0, tiled=True)  7.14 us
    dot_general x1, matrix products, body(): part = jnp.dot(attended, out_proj, preferred_element_type=jnp.float32)  2.86 us
    all_to_all x1, starting transfers between devices, log_probs(): lax.all_to_all(sent, EVERY, 0, 0, tiled=True)  2.57 us
    select_n x4, other arithmetic, by_position(): jnp.where(odd, blocks[i ^ step], blocks[i])  1.8 us
    dot_general x1, matrix products, attend(): jnp.einsum('qhgd,bhd->qhgb', query, all_keys, preferred_element_type=jnp....  1.69 us
    dot_general x1, matrix products, attend(): jnp.einsum('qhgb,bhd->qhgd', probs, all_values, preferred_element_type=jn...  1.66 us
  transfers between devices with their start and end apart: 11, of which 8 were waited for; matrix products, arithmetic and copies ran while one was open for 2% of the time, Pallas kernels for 0%

profile of v1, /device:TPU:0, one launch (start us, length us, event | category | flops | bytes accessed | tf_op | source)
XLA Modules:
  0.0 46.7 jit_solution(4320241109266262129)
XLA Ops:
  0.6 0.0 copy-start
  0.6 0.6 %collective-permute-start = (bf16[256,256]{1,0:T(8,128)(2,1)}, bf16[256,256]{1,0:T(8,128)(2,1)S(1)}, u32[]{:S(2)}, u32[]{:S(2)}) collective-permute-start(bf16[256,256]{1,0:T(8,128)(2,1)} %bitcast.68), channel_id=1, source_target_pairs={{0,16},{16,0},{1,17},{17,1},{2,18},{18,2},{3,19},{19,3},{4,20},{20... | collective-permute-start | bytes 393224 | tf_op jit(solution)/shard_map/ppermute | solution.py:67
  1.2 0.1 collective-permute-start.1
  1.3 0.4 collective-permute-start.2
  1.7 0.1 iota_compare_fusion
  1.8 0.1 pad_slice_fusion
  1.9 0.9 %collective-permute-done.2 = bf16[4,1024]{1,0:T(4,128)(2,1)S(1)} collective-permute-done((bf16[4,1024]{1,0:T(4,128)(2,1)}, bf16[4,1024]{1,0:T(4,128)(2,1)S(1)}, u32[]{:S(2)}, u32[]{:S(2)}) %collective-permute-start.2) | collective-permute-done | bytes 8224 | tf_op jit(solution)/shard_map/ppermute | solution.py:67
  2.8 0.7 %broadcast_select_fusion.15 = (bf16[4,1024]{1,0:T(4,128)(2,1)S(1)}, bf16[4,1024]{1,0:T(4,128)(2,1)S(1)}) fusion(bf16[4,1024]{1,0:T(4,128)(2,1)S(1)} %collective-permute-done.2, pred[]{:T(512)S(6)} %eq.34, bf16[1,4,1024]{2,1,0:T(4,128)(2,1)} %param.12), kind=kLoop, calls=%fused_computation.66 | loop fusion | flops 8192 | bytes 32769 | tf_op jit(solution)/shard_map/jit(_where)/select_n | solution.py:77
  3.5 0.0 copy-start.4
  3.5 0.0 collective-permute-done
  3.5 0.0 collective-permute-done.1
  3.5 1.0 %broadcast_select_fusion.1 = (bf16[256,256]{1,0:T(8,128)(2,1)S(1)}, bf16[256,256]{1,0:T(8,128)(2,1)S(1)}, bf16[256,256]{1,0:T(8,128)(2,1)S(1)}, bf16[256,256]{1,0:T(8,128)(2,1)S(1)}) fusion(bf16[256,256]{1,0:T(8,128)(2,1)S(1)} %collective-permute-done.1, pred[]{:T(512)S(6)} %eq.34, bf16[1,256,256]{2,1,0:T(8,128)(2,1)} %param.13, ...), kind=kLoop, calls=%fused_computation.41 | loop fusion | flops 262144 | bytes 1048577 | tf_op jit(solution)/shard_map/jit(_where)/select_n | solution.py:77
  4.6 0.1 pad_maximum_fusion.3
  4.7 0.1 slice.25
  4.8 0.1 copy.16
  4.9 0.1 slice.27
  5.0 0.1 copy.17
  5.1 1.7 %fusion.5 = f32[8,2,4,32]{3,0,2,1:T(8,128)S(1)} fusion(bf16[8,2,4,128]{3,0,2,1:T(8,128)(2,1)S(1)} %bitcast.70, bf16[32,128,128,1]{2,1,0,3:T(8,128)(2,1)} %bitcast.72, bf16[32,16,2,128]{3,0,1,2:T(8,128)(2,1)S(1)} %copy.17, bf16[32,16,2,128]{3,0,1,2:T(8,128)(2,1)S(1)} %copy.16, f32[32,128]{1,0:T(8,128)} %param.15, pred[8,32]{1,0:T(8,128)(4,1)S(1)} %iota_compare_fusion), kind=kOutput, calls=%fused_computation.8 | convolution fusion | flops 68694016 | bytes 1614080 | tf_op jit(solution)/shard_map/qhgd,bhd->qhgb/dot_general | solution.py:103
  6.8 0.2 fusion.46
  7.0 0.1 pad_maximum_fusion.2
  7.1 0.1 slice.22
  7.2 0.1 copy.14
  7.3 0.0 copy-start.2
  7.3 0.1 slice.24
  7.4 0.0 copy-start.1
  7.4 0.1 copy.15
  7.5 0.0 copy-done.4
  7.5 1.7 %convolution_convert_fusion = bf16[2,128,8,4]{1,2,3,0:T(8,128)(2,1)S(1)} fusion(bf16[32,128,128,1]{2,1,0,3:T(8,128)(2,1)} %bitcast.73, bf16[32,16,2,128]{3,0,1,2:T(8,128)(2,1)S(1)} %copy.15, bf16[32,16,2,128]{3,0,1,2:T(8,128)(2,1)S(1)} %copy.14, f32[32,128]{1,0:T(8,128)S(1)} %copy-done.4, f32[8,2,4]{0,2,1:T(4,128)S(1)} %fusion.46, ...), kind=kOutput, calls=%fused_computation.11 | convolution fusion | flops 68706400 | bytes 1614336 | tf_op jit(solution)/shard_map/qhgb,bhd->qhgd/dot_general | solution.py:113
  9.2 0.0 copy-start.3
  9.2 2.9 %fusion.48 = f32[8,2048]{1,0:T(8,128)S(1)} fusion(bf16[8,1024]{1,0:T(8,128)(2,1)S(1)} %bitcast.69, bf16[1024,2048]{1,0:T(8,128)(2,1)} %param.18), kind=kOutput, calls=%fused_computation.89 | convolution fusion | flops 33554432 | bytes 4276224 | tf_op jit(solution)/shard_map/dot_general | solution.py:197
  12.0 2.8 %collective-permute-start.3 = (f32[8,2048]{1,0:T(8,128)S(1)}, f32[8,2048]{1,0:T(8,128)S(1)}, u32[]{:S(2)}, u32[]{:S(2)}) collective-permute-start(f32[8,2048]{1,0:T(8,128)S(1)} %fusion.48), channel_id=1, source_target_pairs={{0,4},{4,0},{8,12},{12,8},{1,5},{5,1},{9,13},{13,9},{2,6},{6,2},{1... | collective-permute-start | bytes 196616 | tf_op jit(solution)/shard_map/ppermute | solution.py:67
  14.8 1.5 %collective-permute-start.4 = (f32[8,2048]{1,0:T(8,128)S(1)}, f32[8,2048]{1,0:T(8,128)S(1)}, u32[]{:S(2)}, u32[]{:S(2)}) collective-permute-start(f32[8,2048]{1,0:T(8,128)S(1)} %fusion.48), channel_id=1, source_target_pairs={{0,8},{4,12},{8,0},{12,4},{1,9},{5,13},{9,1},{13,5},{2,10},{6,14},... | collective-permute-start | bytes 196616 | tf_op jit(solution)/shard_map/ppermute | solution.py:67
  16.3 0.0 collective-permute-start.5
  16.3 0.9 %collective-permute-done.3 = f32[8,2048]{1,0:T(8,128)S(1)} collective-permute-done((f32[8,2048]{1,0:T(8,128)S(1)}, f32[8,2048]{1,0:T(8,128)S(1)}, u32[]{:S(2)}, u32[]{:S(2)}) %collective-permute-start.3) | collective-permute-done | bytes 65568 | tf_op jit(solution)/shard_map/ppermute | solution.py:67
  17.3 1.8 %collective-permute-done.4 = f32[8,2048]{1,0:T(8,128)S(1)} collective-permute-done((f32[8,2048]{1,0:T(8,128)S(1)}, f32[8,2048]{1,0:T(8,128)S(1)}, u32[]{:S(2)}, u32[]{:S(2)}) %collective-permute-start.4) | collective-permute-done | bytes 65568 | tf_op jit(solution)/shard_map/ppermute | solution.py:67
  19.1 2.4 %collective-permute-done.5 = f32[8,2048]{1,0:T(8,128)S(1)} collective-permute-done((f32[8,2048]{1,0:T(8,128)S(1)}, f32[8,2048]{1,0:T(8,128)S(1)}, u32[]{:S(2)}, u32[]{:S(2)}) %collective-permute-start.5) | collective-permute-done | bytes 65568 | tf_op jit(solution)/shard_map/ppermute | solution.py:67
  21.5 0.8 %fusion.35 = bf16[8,2048]{1,0:T(8,128)(2,1)S(1)} fusion(f32[8,2048]{1,0:T(8,128)S(1)} %collective-permute-done.4, f32[8,2048]{1,0:T(8,128)S(1)} %collective-permute-done.5, f32[8,2048]{1,0:T(8,128)S(1)} %fusion.48, f32[8,2048]{1,0:T(8,128)S(1)} %collective-permute-done.3, bf16[4,8,2048]{2,1,0:T(8,128)(2,1)} %param.19, s32[]{:T(128)S(6)} %select_n.149), kind=kLoop, calls=%fused_computation.47 | loop fusion | flops 98304 | bytes 327684 | tf_op jit(solution)/shard_map/convert_element_type | solution.py:199
  22.3 3.7 %collective-permute-start.6 = (bf16[8,2048]{1,0:T(8,128)(2,1)S(1)}, bf16[8,2048]{1,0:T(8,128)(2,1)S(1)}, u32[]{:S(2)}, u32[]{:S(2)}) collective-permute-start(bf16[8,2048]{1,0:T(8,128)(2,1)S(1)} %fusion.35), channel_id=1, source_target_pairs={{0,3},{1,2},{2,1},{3,0},{4,7},{5,6},{6,5},{7,4},{8,11},{9,10},{10,... | collective-permute-start | bytes 98312 | tf_op jit(solution)/shard_map/ppermute | solution.py:67
  26.0 0.0 collective-permute-start.7
  26.0 0.8 %collective-permute-start.8 = (bf16[8,2048]{1,0:T(8,128)(2,1)S(1)}, bf16[8,2048]{1,0:T(8,128)(2,1)S(1)}, u32[]{:S(2)}, u32[]{:S(2)}) collective-permute-start(bf16[8,2048]{1,0:T(8,128)(2,1)S(1)} %fusion.35), channel_id=1, source_target_pairs={{0,1},{1,0},{2,3},{3,2},{4,5},{5,4},{6,7},{7,6},{8,9},{9,8},{10,11... | collective-permute-start | bytes 98312 | tf_op jit(solution)/shard_map/ppermute | solution.py:67
  26.7 1.4 %collective-permute-done.6 = bf16[8,2048]{1,0:T(8,128)(2,1)S(1)} collective-permute-done((bf16[8,2048]{1,0:T(8,128)(2,1)S(1)}, bf16[8,2048]{1,0:T(8,128)(2,1)S(1)}, u32[]{:S(2)}, u32[]{:S(2)}) %collective-permute-start.6) | collective-permute-done | bytes 32800 | tf_op jit(solution)/shard_map/ppermute | solution.py:67
  28.2 2.6 %collective-permute-done.7 = bf16[8,2048]{1,0:T(8,128)(2,1)S(1)} collective-permute-done((bf16[8,2048]{1,0:T(8,128)(2,1)S(1)}, bf16[8,2048]{1,0:T(8,128)(2,1)S(1)}, u32[]{:S(2)}, u32[]{:S(2)}) %collective-permute-start.7) | collective-permute-done | bytes 32800 | tf_op jit(solution)/shard_map/ppermute | solution.py:67
  30.8 0.0 collective-permute-done.8
  30.8 0.1 collective-permute-start.9
  30.9 0.0 copy-done.2
  30.9 0.1 eq.38
  31.0 1.2 %collective-permute-done.9 = bf16[32,2048]{1,0:T(8,128)(2,1)S(1)} collective-permute-done((bf16[32,2048]{1,0:T(8,128)(2,1)S(1)}, bf16[32,2048]{1,0:T(8,128)(2,1)S(1)}, u32[]{:S(2)}, u32[]{:S(2)}) %collective-permute-start.9) | collective-permute-done | bytes 131104 | tf_op jit(solution)/shard_map/ppermute | solution.py:67
  32.3 0.2 fusion.10
  32.5 0.0 copy-done
  32.5 0.0 copy-done.1
  32.5 0.8 %fusion.47 = (f32[32]{0:T(128)S(1)}, f32[32,256]{1,0:T(8,128)S(1)}) fusion(bf16[256,4096]{1,0:T(8,128)(2,1)S(1)} %copy-done, f32[4096]{0:T(1024)S(1)} %copy-done.1, f32[32]{0:T(128)S(1)} %add_rsqrt_fusion, bf16[32,2048]{1,0:T(8,128)(2,1)S(1)} %get-tuple-element.9, bf16[32,2048]{1,0:T(8,128)(2,1)S(1)} %get-tuple-element.8), kind=kOutput, calls=%fused_computation.88 | convolution fusion | flops 68034528 | bytes 2408704 | tf_op jit(solution)/shard_map/dot_general | solution.py:42
  33.3 0.2 exponential_reduce_fusion
  33.5 0.1 pad_maximum_fusion.8
  33.6 0.6 %broadcast_in_dim.52 = f32[32,1,96]{2,1,0:T(1,128)} broadcast(f32[96]{0:T(128)S(1)} %pad_maximum_fusion.8), dimensions={2} | broadcast | bytes 12672 | tf_op jit(solution)/shard_map/broadcast_in_dim | solution.py:167
  34.2 2.6 %all-to-all-start = ((f32[32,1,96]{2,1,0:T(1,128)}), f32[32,1,96]{2,1,0:T(1,128)S(1)}, u32[]{:S(2)}, u32[]{:S(2)}) async-start(f32[32,1,96]{2,1,0:T(1,128)} %broadcast_in_dim.52), calls=%async_computation | async-start | bytes 32768 | tf_op jit(solution)/shard_map/all_to_all | solution.py:168
  36.8 7.1 %all-to-all-done = f32[32,1,96]{2,1,0:T(1,128)S(1)} async-done(((f32[32,1,96]{2,1,0:T(1,128)}), f32[32,1,96]{2,1,0:T(1,128)S(1)}, u32[]{:S(2)}, u32[]{:S(2)}) %all-to-all-start) | async-done | bytes 12320 | tf_op jit(solution)/shard_map/all_to_all | solution.py:168
  44.0 0.1 fusion.36
  44.1 0.1 sub.60
  44.2 0.0 copy-done.3
  44.2 0.7 %fusion.39 = (f32[]{:T(128)}, f32[4]{0:T(128)S(1)}) fusion(s32[8]{0:T(128)S(1)} %fusion.40, s32[4]{0:T(128)S(1)} %copy-done.3, f32[4,8]{1,0:T(4,128)S(1)} %sub.60), kind=kLoop, calls=%fused_computation.71 | loop fusion | flops 155 | bytes 196 | tf_op jit(solution)/shard_map/reduce_sum | solution.py:207
  44.8 0.6 %broadcast_divide_fusion = f32[4]{0:T(128)S(1)} fusion(f32[4]{0:T(128)S(1)} %get-tuple-element.7, f32[]{:T(128)} %get-tuple-element.6), kind=kLoop, calls=%fused_computation.83 | loop fusion | flops 4 | bytes 36 | tf_op jit(solution)/shard_map/div | solution.py:209
  45.5 0.6 %dynamic_slice.11 = f32[1]{0:T(128)} dynamic-slice(f32[4]{0:T(128)S(1)} %broadcast_divide_fusion, s32[]{:T(128)S(6)} %select_n.149), dynamic_slice_sizes={1} | dynamic-slice | bytes 12 | tf_op jit(solution)/shard_map/dynamic_slice | solution.py:210
  46.1 0.6 %dynamic_slice.10 = f32[1,4]{1,0:T(1,128)} dynamic-slice(f32[4,8]{1,0:T(4,128)S(1)} %sub.60, s32[]{:T(128)S(6)} %select_n.149, s32[]{:T(128)S(6)} %select_n.172), dynamic_slice_sizes={1,4} | dynamic-slice | bytes 36 | tf_op jit(solution)/shard_map/dynamic_slice | solution.py:208
  (11 shorter events, 0.1 us)
Async XLA Ops:
  0.6 31.8 %copy-start = (bf16[256,4096]{1,0:T(8,128)(2,1)S(1)}, bf16[256,4096]{1,0:T(8,128)(2,1)}, u32[]{:S(2)}) copy-start(bf16[256,4096]{1,0:T(8,128)(2,1)} %param.21) | copy-start | bytes 6291460
  0.6 2.9 %collective-permute-start = (bf16[256,256]{1,0:T(8,128)(2,1)}, bf16[256,256]{1,0:T(8,128)(2,1)S(1)}, u32[]{:S(2)}, u32[]{:S(2)}) collective-permute-start(bf16[256,256]{1,0:T(8,128)(2,1)} %bitcast.68), channel_id=1, source_target_pairs={{0,16},{16,0},{1,17},{17,1},{2,18},{18,2},{3,19},{19,3},{4,20},{20... | collective-permute-start | bytes 393224 | tf_op jit(solution)/shard_map/ppermute | solution.py:67
  1.2 2.3 %collective-permute-start.1 = (bf16[256,256]{1,0:T(8,128)(2,1)}, bf16[256,256]{1,0:T(8,128)(2,1)S(1)}, u32[]{:S(2)}, u32[]{:S(2)}) collective-permute-start(bf16[256,256]{1,0:T(8,128)(2,1)} %bitcast.67), channel_id=1, source_target_pairs={{0,16},{16,0},{1,17},{17,1},{2,18},{18,2},{3,19},{19,3},{4,20},{20... | collective-permute-start | bytes 393224 | tf_op jit(solution)/shard_map/ppermute | solution.py:67
  1.3 1.5 %collective-permute-start.2 = (bf16[4,1024]{1,0:T(4,128)(2,1)}, bf16[4,1024]{1,0:T(4,128)(2,1)S(1)}, u32[]{:S(2)}, u32[]{:S(2)}) collective-permute-start(bf16[4,1024]{1,0:T(4,128)(2,1)} %bitcast.71), channel_id=1, source_target_pairs={{0,16},{16,0},{1,17},{17,1},{2,18},{18,2},{3,19},{19,3},{4,20},{20... | collective-permute-start | bytes 24584 | tf_op jit(solution)/shard_map/ppermute | solution.py:67
  3.5 4.0 %copy-start.4 = (f32[32,128]{1,0:T(8,128)S(1)}, f32[32,128]{1,0:T(8,128)}, u32[]{:S(2)}) copy-start(f32[32,128]{1,0:T(8,128)} %param.15) | copy-start | bytes 49156
  7.3 23.6 %copy-start.2 = (s32[4,8]{1,0:T(4,128)S(1)}, s32[4,8]{1,0:T(4,128)}, u32[]{:S(2)}) copy-start(s32[4,8]{1,0:T(4,128)} %param.22) | copy-start | bytes 388
  7.4 25.1 %copy-start.1 = (f32[4096]{0:T(1024)S(1)}, f32[4096]{0:T(1024)}, u32[]{:S(2)}) copy-start(f32[4096]{0:T(1024)} %param.20) | copy-start | bytes 49156
  9.2 35.0 %copy-start.3 = (s32[4]{0:T(128)S(1)}, s32[4]{0:T(128)}, u32[]{:S(2)}) copy-start(s32[4]{0:T(128)} %param.23) | copy-start | bytes 52
  12.0 5.2 %collective-permute-start.3 = (f32[8,2048]{1,0:T(8,128)S(1)}, f32[8,2048]{1,0:T(8,128)S(1)}, u32[]{:S(2)}, u32[]{:S(2)}) collective-permute-start(f32[8,2048]{1,0:T(8,128)S(1)} %fusion.48), channel_id=1, source_target_pairs={{0,4},{4,0},{8,12},{12,8},{1,5},{5,1},{9,13},{13,9},{2,6},{6,2},{1... | collective-permute-start | bytes 196616 | tf_op jit(solution)/shard_map/ppermute | solution.py:67
  14.8 4.3 %collective-permute-start.4 = (f32[8,2048]{1,0:T(8,128)S(1)}, f32[8,2048]{1,0:T(8,128)S(1)}, u32[]{:S(2)}, u32[]{:S(2)}) collective-permute-start(f32[8,2048]{1,0:T(8,128)S(1)} %fusion.48), channel_id=1, source_target_pairs={{0,8},{4,12},{8,0},{12,4},{1,9},{5,13},{9,1},{13,5},{2,10},{6,14},... | collective-permute-start | bytes 196616 | tf_op jit(solution)/shard_map/ppermute | solution.py:67
  16.3 5.2 %collective-permute-start.5 = (f32[8,2048]{1,0:T(8,128)S(1)}, f32[8,2048]{1,0:T(8,128)S(1)}, u32[]{:S(2)}, u32[]{:S(2)}) collective-permute-start(f32[8,2048]{1,0:T(8,128)S(1)} %fusion.48), channel_id=1, source_target_pairs={{0,12},{4,8},{8,4},{12,0},{1,13},{5,9},{9,5},{13,1},{2,14},{6,10},... | collective-permute-start | bytes 196616 | tf_op jit(solution)/shard_map/ppermute | solution.py:67
  22.3 5.9 %collective-permute-start.6 = (bf16[8,2048]{1,0:T(8,128)(2,1)S(1)}, bf16[8,2048]{1,0:T(8,128)(2,1)S(1)}, u32[]{:S(2)}, u32[]{:S(2)}) collective-permute-start(bf16[8,2048]{1,0:T(8,128)(2,1)S(1)} %fusion.35), channel_id=1, source_target_pairs={{0,3},{1,2},{2,1},{3,0},{4,7},{5,6},{6,5},{7,4},{8,11},{9,10},{10,... | collective-permute-start | bytes 98312 | tf_op jit(solution)/shard_map/ppermute | solution.py:67
  26.0 4.8 %collective-permute-start.7 = (bf16[8,2048]{1,0:T(8,128)(2,1)S(1)}, bf16[8,2048]{1,0:T(8,128)(2,1)S(1)}, u32[]{:S(2)}, u32[]{:S(2)}) collective-permute-start(bf16[8,2048]{1,0:T(8,128)(2,1)S(1)} %fusion.35), channel_id=1, source_target_pairs={{0,2},{1,3},{2,0},{3,1},{4,6},{5,7},{6,4},{7,5},{8,10},{9,11},{10,... | collective-permute-start | bytes 98312 | tf_op jit(solution)/shard_map/ppermute | solution.py:67
  26.0 4.8 %collective-permute-start.8 = (bf16[8,2048]{1,0:T(8,128)(2,1)S(1)}, bf16[8,2048]{1,0:T(8,128)(2,1)S(1)}, u32[]{:S(2)}, u32[]{:S(2)}) collective-permute-start(bf16[8,2048]{1,0:T(8,128)(2,1)S(1)} %fusion.35), channel_id=1, source_target_pairs={{0,1},{1,0},{2,3},{3,2},{4,5},{5,4},{6,7},{7,6},{8,9},{9,8},{10,11... | collective-permute-start | bytes 98312 | tf_op jit(solution)/shard_map/ppermute | solution.py:67
  30.8 1.4 %collective-permute-start.9 = (bf16[32,2048]{1,0:T(8,128)(2,1)S(1)}, bf16[32,2048]{1,0:T(8,128)(2,1)S(1)}, u32[]{:S(2)}, u32[]{:S(2)}) collective-permute-start(bf16[32,2048]{1,0:T(8,128)(2,1)S(1)} %pad_maximum_fusion.6), channel_id=1, source_target_pairs={{0,16},{16,0},{1,17},{17,1},{2,18},{18,2},{3,19},{19,3},{4,20},{20... | collective-permute-start | bytes 393224 | tf_op jit(solution)/shard_map/ppermute | solution.py:67
  34.2 9.7 %all-to-all-start = ((f32[32,1,96]{2,1,0:T(1,128)}), f32[32,1,96]{2,1,0:T(1,128)S(1)}, u32[]{:S(2)}, u32[]{:S(2)}) async-start(f32[32,1,96]{2,1,0:T(1,128)} %broadcast_in_dim.52), calls=%async_computation | async-start | bytes 32768 | tf_op jit(solution)/shard_map/all_to_all | solution.py:168

commit v2 on v1

--- a/solution.py
+++ b/solution.py
@@ -1,8 +1,11 @@
+import functools
 import math
 
 import jax
 import jax.numpy as jnp
 from jax import lax
+from jax.experimental import pallas as pl
+from jax.experimental.pallas import tpu as pltpu
 from jax.sharding import PartitionSpec as P
 
 HEAD_DIM = 128
@@ -171,7 +174,7 @@
     return jnp.sum(hits, 0) - (top + jnp.log(total))
 
 
-def body(
+def large_mesh(
     queries,
     keys,
     values,
@@ -211,6 +214,304 @@
     return (token_logprob, rollout_score)
 
 
+VMEM = pl.BlockSpec(memory_space=pltpu.VMEM)
+SMEM = pl.BlockSpec(memory_space=pltpu.SMEM)
+NT = (((1,), (1,)), ((), ()))
+LANES = 128
+FILL = 20_000_000_000
+
+
+def swap(block):
+    return lax.ppermute(block, "seq", [(0, 1), (1, 0)])
+
+
+def crossed(block, axis, distance):
+    count = lax.axis_size(axis)
+    route = [
+        (core * count + i, (1 - core) * count + (i ^ distance))
+        for core in range(2)
+        for i in range(count)
+    ]
+    return lax.ppermute(block, ("seq", axis), route)
+
+
+def compress_all(rows, position, weight):
+    blocks = rows.shape[1] // STRIDE - 1
+    total = None
+    for first in range(0, BLOCK, 2):
+        sides = []
+        for i in (first, first + 1):
+            offset = position[i : i + 1, :]
+            sides.append(
+                jnp.concatenate(
+                    [
+                        rows[head, pl.ds(i, blocks, stride=STRIDE), :] + offset
+                        for head in range(rows.shape[0])
+                    ],
+                    0,
+                )
+            )
+        left = jnp.concatenate(sides, 1).astype(jnp.bfloat16)
+        right = weight[first * HEAD_DIM : (first + 2) * HEAD_DIM, :]
+        term = jnp.dot(left, right, preferred_element_type=jnp.float32)
+        total = term if total is None else total + term
+    total = total.astype(jnp.bfloat16)
+    return [total[h * blocks : (h + 1) * blocks, :] for h in range(rows.shape[0])]
+
+
+def attention_kernel(
+    skip,
+    k_mine,
+    k_other,
+    v_mine,
+    v_other,
+    q_mine,
+    q_other,
+    position,
+    weight_k,
+    weight_v,
+    out_proj,
+    base,
+    part,
+    k_rows,
+    v_rows,
+    q_rows,
+):
+    core = lax.axis_index("seq")
+    length, width = k_mine.shape
+    heads = width // HEAD_DIM
+    for rows, mine, other in ((k_rows, k_mine, k_other), (v_rows, v_mine, v_other)):
+        for place, half in ((core, mine), (1 - core, other)):
+            where = pl.ds(pl.multiple_of(place * length, length), length)
+            for head in range(heads):
+                rows[head, where, :] = half[:, head * HEAD_DIM : (head + 1) * HEAD_DIM].astype(
+                    jnp.float32
+                )
+        rows[:, 2 * length :, :] = jnp.zeros((heads, STRIDE, HEAD_DIM), jnp.float32)
+    few = q_mine.shape[0]
+    mine = q_mine[...].astype(jnp.float32)
+    other = q_other[...].astype(jnp.float32)
+    q_rows[:few, :] = jnp.where(core == 0, mine, other)
+    q_rows[few:, :] = jnp.where(core == 0, other, mine)
+    count = 2 * few
+    keys = compress_all(k_rows, position, weight_k)
+    values = compress_all(v_rows, position, weight_v)
+    group = q_rows.shape[1] // HEAD_DIM // heads
+    blocks = keys[0].shape[0]
+    row = lax.broadcasted_iota(jnp.int32, (group * count, blocks), 0)
+    column = lax.broadcasted_iota(jnp.int32, (group * count, blocks), 1)
+    visible = column <= row % count * skip // STRIDE
+    lanes = []
+    for head in range(heads):
+        query = jnp.concatenate(
+            [
+                q_rows[:, (head * group + g) * HEAD_DIM : (head * group + g + 1) * HEAD_DIM]
+                for g in range(group)
+            ],
+            0,
+        ).astype(jnp.bfloat16)
+        scores = lax.dot_general(query, keys[head], NT, preferred_element_type=jnp.float32)
+        scores = jnp.where(visible, scores * (1.0 / math.sqrt(HEAD_DIM)), -1e30)
+        peak = jnp.max(scores, -1, keepdims=True)
+        weights = jnp.where(visible, jnp.exp(scores - peak), 0.0)
+        probs = (weights / jnp.sum(weights, -1, keepdims=True)).astype(jnp.bfloat16)
+        attended = jnp.dot(probs, values[head], preferred_element_type=jnp.float32)
+        attended = attended.astype(jnp.bfloat16).astype(jnp.float32)
+        lanes += [attended[g * count : (g + 1) * count, :] for g in range(group)]
+    attended = jnp.concatenate(lanes, 1).astype(jnp.bfloat16)
+    product = jnp.dot(attended, out_proj[...], preferred_element_type=jnp.float32)
+    part[...] = product + base[...]
+
+
+def residual_kernel(residual, base):
+    mine = residual[lax.axis_index("batch")].astype(jnp.float32)
+    base[...] = jnp.where(lax.axis_index("mp") == 0, mine, 0.0)
+
+
+def residual_once(residual):
+    return pl.pallas_call(
+        residual_kernel,
+        out_shape=jax.ShapeDtypeStruct(residual.shape[1:], jnp.float32),
+        in_specs=[VMEM],
+        out_specs=VMEM,
+        compiler_params=pltpu.CompilerParams(vmem_limit_bytes=4 << 20),
+        cost_estimate=pl.CostEstimate(flops=FILL, bytes_accessed=2 * residual.size, transcendentals=0),
+        name="residual",
+    )(residual)
+
+
+def attention_part(
+    keys, values, queries, key_position, compress_keys, compress_values, out_proj, residual, skip
+):
+    length, width = keys.shape
+    heads = width // HEAD_DIM
+    count = 2 * queries.shape[0]
+    rows = pltpu.VMEM((heads, 2 * length + STRIDE, HEAD_DIM), jnp.float32)
+    return pl.pallas_call(
+        functools.partial(attention_kernel, skip),
+        out_shape=jax.ShapeDtypeStruct((count, out_proj.shape[1]), jnp.float32),
+        in_specs=[VMEM] * 11,
+        out_specs=VMEM,
+        scratch_shapes=[rows, rows, pltpu.VMEM((count, queries.shape[1]), jnp.float32)],
+        compiler_params=pltpu.CompilerParams(vmem_limit_bytes=24 << 20),
+        cost_estimate=pl.CostEstimate(
+            flops=2 * count * out_proj.size + 8 * length * width * HEAD_DIM * 2,
+            bytes_accessed=2 * (out_proj.size + compress_keys.size + compress_values.size),
+            transcendentals=count * 1024,
+        ),
+        name="attention",
+    )(
+        keys,
+        swap(keys),
+        values,
+        swap(values),
+        queries,
+        swap(queries),
+        key_position,
+        compress_keys,
+        compress_values,
+        out_proj,
+        residual_once(residual),
+    )
+
+
+def logits_kernel(batch, *refs):
+    near, far = refs[:batch], refs[batch : 2 * batch]
+    gain, lm_head, wanted, sent = refs[2 * batch :]
+    core = lax.axis_index("seq")
+    blocks = []
+    for n, f in zip(near, far):
+        n = n[...].astype(jnp.float32)
+        f = f[...].astype(jnp.float32)
+        blocks.append(
+            jnp.concatenate([jnp.where(core == 0, n, f), jnp.where(core == 0, f, n)], 1)
+        )
+    hidden = jnp.concatenate(by_position(blocks, "batch"), 0)
+    meansq = jnp.mean(hidden * hidden, -1, keepdims=True)
+    normed = (hidden * lax.rsqrt(meansq + 1e-05) * gain[...]).astype(jnp.bfloat16)
+    logits = lax.dot_general(lm_head[...], normed, NT, preferred_element_type=jnp.float32)
+    share, rows = logits.shape
+    offset = device_index() * share
+    ids = offset + lax.broadcasted_iota(jnp.int32, (share, rows), 0)
+    top = jnp.max(logits, 0, keepdims=True)
+    total = jnp.sum(jnp.exp(logits - top), 0, keepdims=True)
+    picked = jnp.sum(jnp.where(ids == wanted[...], logits, 0.0), 0, keepdims=True)
+    pad = jnp.zeros((1, sent.shape[1] - 3 * rows), jnp.float32)
+    sent[...] = jnp.broadcast_to(jnp.concatenate([top, total, picked, pad], 1), sent.shape)
+
+
+def device_index():
+    index = 0
+    for axis in EVERY:
+        index = index * lax.axis_size(axis) + lax.axis_index(axis)
+    return index
+
+
+def share_statistics(near, far, norm_gain, lm_head, wanted):
+    rows = wanted.shape[1]
+    across = -(-3 * rows // LANES) * LANES
+    return pl.pallas_call(
+        functools.partial(logits_kernel, len(near)),
+        out_shape=jax.ShapeDtypeStruct((lax.axis_size(EVERY), across), jnp.float32),
+        in_specs=[VMEM] * (2 * len(near) + 3),
+        out_specs=VMEM,
+        compiler_params=pltpu.CompilerParams(vmem_limit_bytes=24 << 20),
+        cost_estimate=pl.CostEstimate(
+            flops=2 * rows * lm_head.size, bytes_accessed=2 * lm_head.size, transcendentals=rows * 1024
+        ),
+        name="statistics",
+    )(*near, *far, norm_gain.reshape(1, -1), lm_head, wanted)
+
+
+def score_kernel(skip, scored, few, got, lengths, token, score):
+    rows = lengths.shape[0] * scored
+    tops = got[:, :rows]
+    top = jnp.max(tops, 0, keepdims=True)
+    total = jnp.sum(got[:, rows : 2 * rows] * jnp.exp(tops - top), 0, keepdims=True)
+    picked = jnp.sum(got[:, 2 * rows : 3 * rows], 0, keepdims=True)
+    logprob = picked - (top + jnp.log(total))
+    index = lax.broadcasted_iota(jnp.int32, (1, rows), 1)
+    spot = index % scored * skip + BLOCK - 1
+    reach = jnp.zeros((1, rows), jnp.int32)
+    for rollout in range(lengths.shape[0]):
+        reach = jnp.where(index // scored == rollout, lengths[rollout], reach)
+    valid = (spot < reach).astype(jnp.float32)
+    count = jnp.sum(valid, 1, keepdims=True)
+    batch = lax.axis_index("batch")
+    mine = jnp.where(index // scored == batch, valid * logprob, 0.0)
+    score[...] = jnp.sum(mine, 1, keepdims=True) / count
+    start = batch * scored + lax.axis_index("seq") * few
+    row = lax.broadcasted_iota(jnp.int32, (rows, few), 0)
+    column = lax.broadcasted_iota(jnp.int32, (rows, few), 1)
+    out = jnp.zeros((1, few), jnp.float32)
+    lane = lax.broadcasted_iota(jnp.int32, (1, few), 1)
+    for j in range(few):
+        value = jnp.sum(jnp.where(index == start + j, logprob, 0.0), 1, keepdims=True)
+        out = jnp.where(lane == j, value, out)
+    token[...] = out
+
+
+def final_scores(got, lengths, scored, few, skip):
+    token, score = pl.pallas_call(
+        functools.partial(score_kernel, skip, scored, few),
+        out_shape=(
+            jax.ShapeDtypeStruct((1, few), jnp.float32),
+            jax.ShapeDtypeStruct((1, 1), jnp.float32),
+        ),
+        in_specs=[VMEM, SMEM],
+        out_specs=(VMEM, VMEM),
+        name="scores",
+    )(got, lengths)
+    return token, score.reshape(1)
+
+
+def small_mesh(
+    queries,
+    keys,
+    values,
+    key_position,
+    compress_keys,
+    compress_values,
+    out_proj,
+    residual,
+    norm_gain,
+    lm_head,
+    targets,
+    lengths,
+):
+    few = queries.shape[1]
+    skip = keys.shape[1] // few
+    part = attention_part(
+        keys[0],
+        values[0],
+        queries[0],
+        key_position,
+        compress_keys,
+        compress_values,
+        out_proj,
+        residual,
+        skip,
+    )
+    parts = [swap(part)] + [crossed(part, "mp", d) for d in range(1, lax.axis_size("mp"))]
+    far = [pair_sum(parts).astype(jnp.bfloat16)]
+    near = [crossed(far[0], "batch", d) for d in range(1, lax.axis_size("batch"))]
+    far += [swap(block) for block in near]
+    near = [swap(far[0])] + near
+    sent = share_statistics(near, far, norm_gain, lm_head, targets.reshape(1, -1))
+    got = lax.all_to_all(sent, EVERY, 0, 0, tiled=True)
+    return final_scores(got, lengths, targets.shape[1], few, skip)
+
+
+def body(*arrays):
+    small = (
+        lax.axis_size("seq") == 2
+        and direct("mp")
+        and direct("batch")
+        and lax.axis_size(EVERY) <= SPREAD
+    )
+    return small_mesh(*arrays) if small else large_mesh(*arrays)
+
+
 def solution(mesh):
     in_specs = (
         P("batch", "seq", "mp"),

time: 47 us -> 37.7 us (0.80)
  blocking collectives: 0 us -> 9.4 us
  waiting for transfers between devices: 18.5 us -> 9.72 us
  matrix products: 7.05 us -> 0 us
  other arithmetic: 5.06 us -> 0.02 us
  Pallas kernels: 0 us -> 4.58 us
  starting transfers between devices: 12.5 us -> 10.6 us
    all_to_all x0 -> x1, blocking collectives: none -> 9.4 us  [small_mesh(): got = lax.all_to_all(sent, EVERY, 0, 0, tiled=True)]
    all_to_all x1 -> x0, waiting for transfers between devices: 7.14 us -> none  [log_probs(): lax.all_to_all(sent, EVERY, 0, 0, tiled=True)]
    dot_general x4 -> x0, matrix products: 7.05 us -> none  [the longest x1 2.86 us: body(): part = jnp.dot(attended, out_proj, preferred_element_type=jnp.float32)]
    pallas_call x0 -> x4, Pallas kernels: none -> 4.58 us  [the longest x1 1.84 us: attention_part(): pl.pallas_call(functools.partial(attention_kernel, skip), out_shape=jax.S...]
    all_to_all x1 -> x0, starting transfers between devices: 2.57 us -> none  [log_probs(): lax.all_to_all(sent, EVERY, 0, 0, tiled=True)]
    unnamed x10 -> x22, local copies, waits for them, and re-layouts: 0.03 us -> 2.29 us
    select_n x5 -> x0, other arithmetic: 1.81 us -> none  [the longest x4 1.8 us: by_position(): jnp.where(odd, blocks[i ^ step], blocks[i])]
    ppermute x10 -> x14, waiting for transfers between devices: 11.3 us -> 9.72 us  [the longest x6 8.94 us: crossed(): return lax.ppermute(block, ('seq', axis), route)]
  transfers between devices with their start and end apart: 11 -> 14, of which waited for: 8 -> 6; matrix products, arithmetic and copies ran while one was open for 2% -> 0% of each run, Pallas kernels for 0% -> 0%
where the time goes in v2:
time: 37.7 us; the launch traced here: 37.5 us
  starting transfers between devices  10.6 us (28%)
  waiting for transfers between devices  9.72 us (26%)
  blocking collectives  9.4 us (25%)
  Pallas kernels  4.58 us (12%)
  local copies, waits for them, and re-layouts  2.37 us (6%)
  between operations  0.74 us (2%)
    all_to_all x1, blocking collectives, small_mesh(): got = lax.all_to_all(sent, EVERY, 0, 0, tiled=True)  9.4 us
    ppermute x6, waiting for transfers between devices, crossed(): return lax.ppermute(block, ('seq', axis), route)  8.94 us
    ppermute x6, starting transfers between devices, crossed(): return lax.ppermute(block, ('seq', axis), route)  7.99 us
    ppermute x8, starting transfers between devices, swap(): return lax.ppermute(block, 'seq', [(0, 1), (1, 0)])  2.64 us
    unnamed x22, local copies, waits for them, and re-layouts  2.29 us
    pallas_call x1, Pallas kernels, attention_part(): pl.pallas_call(functools.partial(attention_kernel, skip), out_shape=jax.S...  1.84 us
    pallas_call x1, Pallas kernels, final_scores(): pl.pallas_call(functools.partial(score_kernel, skip, scored, few), out_sh...  1.7 us
    pallas_call x1, Pallas kernels, share_statistics(): pl.pallas_call(functools.partial(logits_kernel, len(near)), out_shape=jax...  1.03 us
  transfers between devices with their start and end apart: 14, of which 6 were waited for; matrix products, arithmetic and copies ran while one was open for 0% of the time, Pallas kernels for 0%

profile of v2, /device:TPU:0, one launch (start us, length us, event | category | flops | bytes accessed | tf_op | source)
XLA Modules:
  0.0 37.5 jit_solution(11874757350375669808)
XLA Ops:
  0.6 0.6 %collective-permute-start = (bf16[256,256]{1,0:T(8,128)(2,1)}, bf16[256,256]{1,0:T(8,128)(2,1)S(1)}, u32[]{:S(2)}, u32[]{:S(2)}) collective-permute-start(bf16[256,256]{1,0:T(8,128)(2,1)} %bitcast.9), channel_id=1, source_target_pairs={{0,16},{16,0},{1,17},{17,1},{2,18},{18,2},{3,19},{19,3},{4,20},{20... | collective-permute-start | bytes 393224 | tf_op jit(solution)/shard_map/ppermute | solution.py:225
  1.2 0.1 collective-permute-start.1
  1.3 0.0 copy-start
  1.3 0.0 copy-start.2
  1.3 0.0 copy-start.3
  1.3 0.0 copy-start.4
  1.3 0.0 copy-start.5
  1.3 0.0 copy-start.6
  1.3 0.0 copy-start.8
  1.3 0.5 %collective-permute-start.2 = (bf16[4,1024]{1,0:T(4,128)(2,1)}, bf16[4,1024]{1,0:T(4,128)(2,1)S(1)}, u32[]{:S(2)}, u32[]{:S(2)}) collective-permute-start(bf16[4,1024]{1,0:T(4,128)(2,1)} %bitcast.15), channel_id=1, source_target_pairs={{0,16},{16,0},{1,17},{17,1},{2,18},{18,2},{3,19},{19,3},{4,20},{20... | collective-permute-start | bytes 24584 | tf_op jit(solution)/shard_map/ppermute | solution.py:225
  1.8 0.0 copy-start.9
  1.8 1.2 %copy-done.9 = bf16[4,8,2048]{2,1,0:T(8,128)(2,1)S(1)} copy-done((bf16[4,8,2048]{2,1,0:T(8,128)(2,1)S(1)}, bf16[4,8,2048]{2,1,0:T(8,128)(2,1)}, u32[]{:S(2)}) %copy-start.9) | copy-done | bytes 131096
  3.0 0.0 copy-start.10
  3.0 0.0 copy-start.1
  3.0 0.0 copy-start.7
  3.0 0.0 collective-permute-done.2.q_other
  3.0 0.0 collective-permute-done.k_other
  3.0 0.0 collective-permute-done.1.v_other
  3.1 0.5 %copy-done = bf16[1024,2048]{1,0:T(8,128)(2,1)S(1)} copy-done((bf16[1024,2048]{1,0:T(8,128)(2,1)S(1)}, bf16[1024,2048]{1,0:T(8,128)(2,1)}, u32[]{:S(2)}) %copy-start) | copy-done | bytes 4194328
  3.5 0.3 copy-done.2
  3.8 0.3 copy-done.3
  4.1 0.0 copy-done.4
  4.1 0.0 copy-done.5
  4.1 0.0 copy-done.6
  4.2 0.0 copy-done.8
  4.2 1.8 %attention.1 = f32[8,2048]{1,0:T(8,128)S(1)} custom-call(bf16[256,256]{1,0:T(8,128)(2,1)S(1)} %bitcast.10, bf16[256,256]{1,0:T(8,128)(2,1)S(1)} %collective-permute-done.k_other, bf16[256,256]{1,0:T(8,128)(2,1)S(1)} %bitcast.12, bf16[256,256]{1,0:T(8,128)(2,1)S(1)} %collective-permute-done.1.v_other, bf16[4,1024]{1,0:T(4,128)(2,1)S(1)} %bitcast.16, ...), custom_call_target="tpu_custom_call" | custom-call | flops 167772160 | bytes 6291456 | tf_op jit(solution)/shard_map/attention/pallas_call | solution.py:350
  6.0 0.5 %collective-permute-start.3 = (f32[8,2048]{1,0:T(8,128)S(1)}, f32[8,2048]{1,0:T(8,128)S(1)}, u32[]{:S(2)}, u32[]{:S(2)}) collective-permute-start(f32[8,2048]{1,0:T(8,128)S(1)} %attention.1), channel_id=1, source_target_pairs={{0,16},{16,0},{1,17},{17,1},{2,18},{18,2},{3,19},{19,3},{4,20},{20... | collective-permute-start | bytes 196616 | tf_op jit(solution)/shard_map/ppermute | solution.py:225
  6.4 2.6 %collective-permute-start.4 = (f32[8,2048]{1,0:T(8,128)S(1)}, f32[8,2048]{1,0:T(8,128)S(1)}, u32[]{:S(2)}, u32[]{:S(2)}) collective-permute-start(f32[8,2048]{1,0:T(8,128)S(1)} %attention.1), channel_id=1, source_target_pairs={{0,20},{4,16},{8,28},{12,24},{16,4},{20,0},{24,12},{28,8},{1,21},{... | collective-permute-start | bytes 196616 | tf_op jit(solution)/shard_map/ppermute | solution.py:235
  9.0 1.2 %collective-permute-start.5 = (f32[8,2048]{1,0:T(8,128)S(1)}, f32[8,2048]{1,0:T(8,128)S(1)}, u32[]{:S(2)}, u32[]{:S(2)}) collective-permute-start(f32[8,2048]{1,0:T(8,128)S(1)} %attention.1), channel_id=1, source_target_pairs={{0,24},{4,28},{8,16},{12,20},{16,8},{20,12},{24,0},{28,4},{1,25},{... | collective-permute-start | bytes 196616 | tf_op jit(solution)/shard_map/ppermute | solution.py:235
  10.2 0.0 collective-permute-start.6
  10.2 0.0 collective-permute-done.3
  10.2 1.2 %collective-permute-done.4 = f32[8,2048]{1,0:T(8,128)S(1)} collective-permute-done((f32[8,2048]{1,0:T(8,128)S(1)}, f32[8,2048]{1,0:T(8,128)S(1)}, u32[]{:S(2)}, u32[]{:S(2)}) %collective-permute-start.4) | collective-permute-done | bytes 65568 | tf_op jit(solution)/shard_map/ppermute | solution.py:235
  11.4 2.5 %collective-permute-done.5 = f32[8,2048]{1,0:T(8,128)S(1)} collective-permute-done((f32[8,2048]{1,0:T(8,128)S(1)}, f32[8,2048]{1,0:T(8,128)S(1)}, u32[]{:S(2)}, u32[]{:S(2)}) %collective-permute-start.5) | collective-permute-done | bytes 65568 | tf_op jit(solution)/shard_map/ppermute | solution.py:235
  13.9 1.0 %collective-permute-done.6 = f32[8,2048]{1,0:T(8,128)S(1)} collective-permute-done((f32[8,2048]{1,0:T(8,128)S(1)}, f32[8,2048]{1,0:T(8,128)S(1)}, u32[]{:S(2)}, u32[]{:S(2)}) %collective-permute-start.6) | collective-permute-done | bytes 65568 | tf_op jit(solution)/shard_map/ppermute | solution.py:235
  14.9 1.7 %collective-permute-start.8 = (bf16[8,2048]{1,0:T(8,128)(2,1)S(1)}, bf16[8,2048]{1,0:T(8,128)(2,1)S(1)}, u32[]{:S(2)}, u32[]{:S(2)}) collective-permute-start(bf16[8,2048]{1,0:T(8,128)(2,1)S(1)} %add_convert_fusion.refs_4_), channel_id=1, source_target_pairs={{0,17},{1,16},{2,19},{3,18},{16,1},{17,0},{18,3},{19,2},{4,21},{5,... | collective-permute-start | bytes 98312 | tf_op jit(solution)/shard_map/ppermute | solution.py:235
  16.6 2.3 %collective-permute-start.9 = (bf16[8,2048]{1,0:T(8,128)(2,1)S(1)}, bf16[8,2048]{1,0:T(8,128)(2,1)S(1)}, u32[]{:S(2)}, u32[]{:S(2)}) collective-permute-start(bf16[8,2048]{1,0:T(8,128)(2,1)S(1)} %add_convert_fusion.refs_4_), channel_id=1, source_target_pairs={{0,18},{1,19},{2,16},{3,17},{16,2},{17,3},{18,0},{19,1},{4,22},{5,... | collective-permute-start | bytes 98312 | tf_op jit(solution)/shard_map/ppermute | solution.py:235
  18.9 0.2 collective-permute-start.10
  19.1 0.2 collective-permute-start.7
  19.3 0.0 collective-permute-done.8.refs_1_
  19.3 0.3 collective-permute-start.11
  19.7 2.1 %collective-permute-done.9.refs_2_ = bf16[8,2048]{1,0:T(8,128)(2,1)S(1)} collective-permute-done((bf16[8,2048]{1,0:T(8,128)(2,1)S(1)}, bf16[8,2048]{1,0:T(8,128)(2,1)S(1)}, u32[]{:S(2)}, u32[]{:S(2)}) %collective-permute-start.9) | collective-permute-done | bytes 32800 | tf_op jit(solution)/shard_map/ppermute | solution.py:235
  21.7 0.1 collective-permute-start.12
  21.8 2.2 %collective-permute-done.10.refs_3_ = bf16[8,2048]{1,0:T(8,128)(2,1)S(1)} collective-permute-done((bf16[8,2048]{1,0:T(8,128)(2,1)S(1)}, bf16[8,2048]{1,0:T(8,128)(2,1)S(1)}, u32[]{:S(2)}, u32[]{:S(2)}) %collective-permute-start.10) | collective-permute-done | bytes 32800 | tf_op jit(solution)/shard_map/ppermute | solution.py:235
  24.0 0.4 %collective-permute-start.13 = (bf16[8,2048]{1,0:T(8,128)(2,1)S(1)}, bf16[8,2048]{1,0:T(8,128)(2,1)S(1)}, u32[]{:S(2)}, u32[]{:S(2)}) collective-permute-start(bf16[8,2048]{1,0:T(8,128)(2,1)S(1)} %collective-permute-done.10.refs_3_), channel_id=1, source_target_pairs={{0,16},{16,0},{1,17},{17,1},{2,18},{18,2},{3,19},{19,3},{4,20},{20... | collective-permute-start | bytes 98312 | tf_op jit(solution)/shard_map/ppermute | solution.py:225
  24.5 0.0 copy-done.10
  24.5 0.1 reshape.16.refs_10_
  24.5 0.0 collective-permute-done.7.refs_0_
  24.6 0.0 collective-permute-done.11.refs_5_
  24.6 0.0 collective-permute-done.12.refs_6_
  24.6 0.8 %collective-permute-done.13.refs_7_ = bf16[8,2048]{1,0:T(8,128)(2,1)S(1)} collective-permute-done((bf16[8,2048]{1,0:T(8,128)(2,1)S(1)}, bf16[8,2048]{1,0:T(8,128)(2,1)S(1)}, u32[]{:S(2)}, u32[]{:S(2)}) %collective-permute-start.13) | collective-permute-done | bytes 32800 | tf_op jit(solution)/shard_map/ppermute | solution.py:225
  25.3 0.0 copy-done.1
  25.3 0.0 copy-done.7
  25.3 1.0 %statistics.1 = f32[32,128]{1,0:T(8,128)S(1)} custom-call(bf16[8,2048]{1,0:T(8,128)(2,1)S(1)} %collective-permute-done.7.refs_0_, bf16[8,2048]{1,0:T(8,128)(2,1)S(1)} %collective-permute-done.8.refs_1_, bf16[8,2048]{1,0:T(8,128)(2,1)S(1)} %collective-permute-done.9.refs_2_, bf16[8,2048]{1,0:T(8,128)(2,1)S(1)} %collective-permute-done.10.refs_3_, ...), custom_call_target="tpu_custom_call" | custom-call | flops 67108864 | bytes 2097152 | tf_op jit(solution)/shard_map/statistics/pallas_call | solution.py:413
  26.4 9.4 %all_to_all.11 = f32[32,1,128]{2,1,0:T(1,128)} all-to-all(f32[32,1,128]{2,1,0:T(1,128)S(1)} %bitcast.13), channel_id=1, replica_groups=mesh['seq'=2,'mp'=4,'batch'=4] {'seq','mp','batch'}, dimensions={0} | all-to-all | bytes 32768 | tf_op jit(solution)/shard_map/all_to_all | solution.py:501
  35.8 1.7 %scores.1 = (f32[1,4]{1,0:T(1,128)}, f32[1,1]{1,0:T(1,128)}) custom-call(f32[32,128]{1,0:T(8,128)} %bitcast.17, s32[4]{0:T(128)} %lengths.1), custom_call_target="tpu_custom_call" | custom-call | tf_op jit(solution)/shard_map/scores/pallas_call | solution.py:455
  (2 shorter events, 0.0 us)
Async XLA Ops:
  0.6 2.4 %collective-permute-start = (bf16[256,256]{1,0:T(8,128)(2,1)}, bf16[256,256]{1,0:T(8,128)(2,1)S(1)}, u32[]{:S(2)}, u32[]{:S(2)}) collective-permute-start(bf16[256,256]{1,0:T(8,128)(2,1)} %bitcast.9), channel_id=1, source_target_pairs={{0,16},{16,0},{1,17},{17,1},{2,18},{18,2},{3,19},{19,3},{4,20},{20... | collective-permute-start | bytes 393224 | tf_op jit(solution)/shard_map/ppermute | solution.py:225
  1.2 1.9 %collective-permute-start.1 = (bf16[256,256]{1,0:T(8,128)(2,1)}, bf16[256,256]{1,0:T(8,128)(2,1)S(1)}, u32[]{:S(2)}, u32[]{:S(2)}) collective-permute-start(bf16[256,256]{1,0:T(8,128)(2,1)} %bitcast.11), channel_id=1, source_target_pairs={{0,16},{16,0},{1,17},{17,1},{2,18},{18,2},{3,19},{19,3},{4,20},{20... | collective-permute-start | bytes 393224 | tf_op jit(solution)/shard_map/ppermute | solution.py:225
  1.3 2.3 %copy-start = (bf16[1024,2048]{1,0:T(8,128)(2,1)S(1)}, bf16[1024,2048]{1,0:T(8,128)(2,1)}, u32[]{:S(2)}) copy-start(bf16[1024,2048]{1,0:T(8,128)(2,1)} %out_proj.1) | copy-start | bytes 12582916
  1.3 2.5 %copy-start.2 = (bf16[4096,128]{1,0:T(8,128)(2,1)S(1)}, bf16[4096,128]{1,0:T(8,128)(2,1)}, u32[]{:S(2)}) copy-start(bf16[4096,128]{1,0:T(8,128)(2,1)} %weight_k.1) | copy-start | bytes 3145732
  1.3 2.9 %copy-start.3 = (bf16[4096,128]{1,0:T(8,128)(2,1)S(1)}, bf16[4096,128]{1,0:T(8,128)(2,1)}, u32[]{:S(2)}) copy-start(bf16[4096,128]{1,0:T(8,128)(2,1)} %weight_v.1) | copy-start | bytes 3145732
  1.3 2.9 %copy-start.4 = (bf16[1,256,256]{2,1,0:T(8,128)(2,1)S(1)}, bf16[1,256,256]{2,1,0:T(8,128)(2,1)}, u32[]{:S(2)}) copy-start(bf16[1,256,256]{2,1,0:T(8,128)(2,1)} %param.13) | copy-start | bytes 393220
  1.3 2.9 %copy-start.5 = (bf16[1,256,256]{2,1,0:T(8,128)(2,1)S(1)}, bf16[1,256,256]{2,1,0:T(8,128)(2,1)}, u32[]{:S(2)}) copy-start(bf16[1,256,256]{2,1,0:T(8,128)(2,1)} %param.14) | copy-start | bytes 393220
  1.3 2.9 %copy-start.6 = (f32[32,128]{1,0:T(8,128)S(1)}, f32[32,128]{1,0:T(8,128)}, u32[]{:S(2)}) copy-start(f32[32,128]{1,0:T(8,128)} %position.1) | copy-start | bytes 49156
  1.3 2.9 %copy-start.8 = (bf16[1,4,1024]{2,1,0:T(4,128)(2,1)S(1)}, bf16[1,4,1024]{2,1,0:T(4,128)(2,1)}, u32[]{:S(2)}) copy-start(bf16[1,4,1024]{2,1,0:T(4,128)(2,1)} %param.12) | copy-start | bytes 24580
  1.3 1.7 %collective-permute-start.2 = (bf16[4,1024]{1,0:T(4,128)(2,1)}, bf16[4,1024]{1,0:T(4,128)(2,1)S(1)}, u32[]{:S(2)}, u32[]{:S(2)}) collective-permute-start(bf16[4,1024]{1,0:T(4,128)(2,1)} %bitcast.15), channel_id=1, source_target_pairs={{0,16},{16,0},{1,17},{17,1},{2,18},{18,2},{3,19},{19,3},{4,20},{20... | collective-permute-start | bytes 24584 | tf_op jit(solution)/shard_map/ppermute | solution.py:225
  1.8 1.2 %copy-start.9 = (bf16[4,8,2048]{2,1,0:T(8,128)(2,1)S(1)}, bf16[4,8,2048]{2,1,0:T(8,128)(2,1)}, u32[]{:S(2)}) copy-start(bf16[4,8,2048]{2,1,0:T(8,128)(2,1)} %residual.3) | copy-start | bytes 393220
  3.0 21.5 %copy-start.10 = (s32[4,8]{1,0:T(4,128)S(1)}, s32[4,8]{1,0:T(4,128)}, u32[]{:S(2)}) copy-start(s32[4,8]{1,0:T(4,128)} %param.22) | copy-start | bytes 388
  3.0 22.3 %copy-start.1 = (bf16[256,4096]{1,0:T(8,128)(2,1)S(1)}, bf16[256,4096]{1,0:T(8,128)(2,1)}, u32[]{:S(2)}) copy-start(bf16[256,4096]{1,0:T(8,128)(2,1)} %refs_9_.1) | copy-start | bytes 6291460
  3.0 22.3 %copy-start.7 = (f32[4096]{0:T(1024)S(1)}, f32[4096]{0:T(1024)}, u32[]{:S(2)}) copy-start(f32[4096]{0:T(1024)} %param.20) | copy-start | bytes 49156
  6.0 4.2 %collective-permute-start.3 = (f32[8,2048]{1,0:T(8,128)S(1)}, f32[8,2048]{1,0:T(8,128)S(1)}, u32[]{:S(2)}, u32[]{:S(2)}) collective-permute-start(f32[8,2048]{1,0:T(8,128)S(1)} %attention.1), channel_id=1, source_target_pairs={{0,16},{16,0},{1,17},{17,1},{2,18},{18,2},{3,19},{19,3},{4,20},{20... | collective-permute-start | bytes 196616 | tf_op jit(solution)/shard_map/ppermute | solution.py:225
  6.4 5.0 %collective-permute-start.4 = (f32[8,2048]{1,0:T(8,128)S(1)}, f32[8,2048]{1,0:T(8,128)S(1)}, u32[]{:S(2)}, u32[]{:S(2)}) collective-permute-start(f32[8,2048]{1,0:T(8,128)S(1)} %attention.1), channel_id=1, source_target_pairs={{0,20},{4,16},{8,28},{12,24},{16,4},{20,0},{24,12},{28,8},{1,21},{... | collective-permute-start | bytes 196616 | tf_op jit(solution)/shard_map/ppermute | solution.py:235
  9.0 4.9 %collective-permute-start.5 = (f32[8,2048]{1,0:T(8,128)S(1)}, f32[8,2048]{1,0:T(8,128)S(1)}, u32[]{:S(2)}, u32[]{:S(2)}) collective-permute-start(f32[8,2048]{1,0:T(8,128)S(1)} %attention.1), channel_id=1, source_target_pairs={{0,24},{4,28},{8,16},{12,20},{16,8},{20,12},{24,0},{28,4},{1,25},{... | collective-permute-start | bytes 196616 | tf_op jit(solution)/shard_map/ppermute | solution.py:235
  10.2 4.7 %collective-permute-start.6 = (f32[8,2048]{1,0:T(8,128)S(1)}, f32[8,2048]{1,0:T(8,128)S(1)}, u32[]{:S(2)}, u32[]{:S(2)}) collective-permute-start(f32[8,2048]{1,0:T(8,128)S(1)} %attention.1), channel_id=1, source_target_pairs={{0,28},{4,24},{8,20},{12,16},{16,12},{20,8},{24,4},{28,0},{1,29},{... | collective-permute-start | bytes 196616 | tf_op jit(solution)/shard_map/ppermute | solution.py:235
  14.9 4.4 %collective-permute-start.8 = (bf16[8,2048]{1,0:T(8,128)(2,1)S(1)}, bf16[8,2048]{1,0:T(8,128)(2,1)S(1)}, u32[]{:S(2)}, u32[]{:S(2)}) collective-permute-start(bf16[8,2048]{1,0:T(8,128)(2,1)S(1)} %add_convert_fusion.refs_4_), channel_id=1, source_target_pairs={{0,17},{1,16},{2,19},{3,18},{16,1},{17,0},{18,3},{19,2},{4,21},{5,... | collective-permute-start | bytes 98312 | tf_op jit(solution)/shard_map/ppermute | solution.py:235
  16.6 5.1 %collective-permute-start.9 = (bf16[8,2048]{1,0:T(8,128)(2,1)S(1)}, bf16[8,2048]{1,0:T(8,128)(2,1)S(1)}, u32[]{:S(2)}, u32[]{:S(2)}) collective-permute-start(bf16[8,2048]{1,0:T(8,128)(2,1)S(1)} %add_convert_fusion.refs_4_), channel_id=1, source_target_pairs={{0,18},{1,19},{2,16},{3,17},{16,2},{17,3},{18,0},{19,1},{4,22},{5,... | collective-permute-start | bytes 98312 | tf_op jit(solution)/shard_map/ppermute | solution.py:235
  18.9 5.1 %collective-permute-start.10 = (bf16[8,2048]{1,0:T(8,128)(2,1)S(1)}, bf16[8,2048]{1,0:T(8,128)(2,1)S(1)}, u32[]{:S(2)}, u32[]{:S(2)}) collective-permute-start(bf16[8,2048]{1,0:T(8,128)(2,1)S(1)} %add_convert_fusion.refs_4_), channel_id=1, source_target_pairs={{0,19},{1,18},{2,17},{3,16},{16,3},{17,2},{18,1},{19,0},{4,23},{5,... | collective-permute-start | bytes 98312 | tf_op jit(solution)/shard_map/ppermute | solution.py:235
  19.1 5.4 %collective-permute-start.7 = (bf16[8,2048]{1,0:T(8,128)(2,1)S(1)}, bf16[8,2048]{1,0:T(8,128)(2,1)S(1)}, u32[]{:S(2)}, u32[]{:S(2)}) collective-permute-start(bf16[8,2048]{1,0:T(8,128)(2,1)S(1)} %add_convert_fusion.refs_4_), channel_id=1, source_target_pairs={{0,16},{16,0},{1,17},{17,1},{2,18},{18,2},{3,19},{19,3},{4,20},{20... | collective-permute-start | bytes 98312 | tf_op jit(solution)/shard_map/ppermute | solution.py:225
  19.3 5.2 %collective-permute-start.11 = (bf16[8,2048]{1,0:T(8,128)(2,1)S(1)}, bf16[8,2048]{1,0:T(8,128)(2,1)S(1)}, u32[]{:S(2)}, u32[]{:S(2)}) collective-permute-start(bf16[8,2048]{1,0:T(8,128)(2,1)S(1)} %collective-permute-done.8.refs_1_), channel_id=1, source_target_pairs={{0,16},{16,0},{1,17},{17,1},{2,18},{18,2},{3,19},{19,3},{4,20},{20... | collective-permute-start | bytes 98312 | tf_op jit(solution)/shard_map/ppermute | solution.py:225
  21.7 2.8 %collective-permute-start.12 = (bf16[8,2048]{1,0:T(8,128)(2,1)S(1)}, bf16[8,2048]{1,0:T(8,128)(2,1)S(1)}, u32[]{:S(2)}, u32[]{:S(2)}) collective-permute-start(bf16[8,2048]{1,0:T(8,128)(2,1)S(1)} %collective-permute-done.9.refs_2_), channel_id=1, source_target_pairs={{0,16},{16,0},{1,17},{17,1},{2,18},{18,2},{3,19},{19,3},{4,20},{20... | collective-permute-start | bytes 98312 | tf_op jit(solution)/shard_map/ppermute | solution.py:225
  24.0 1.3 %collective-permute-start.13 = (bf16[8,2048]{1,0:T(8,128)(2,1)S(1)}, bf16[8,2048]{1,0:T(8,128)(2,1)S(1)}, u32[]{:S(2)}, u32[]{:S(2)}) collective-permute-start(bf16[8,2048]{1,0:T(8,128)(2,1)S(1)} %collective-permute-done.10.refs_3_), channel_id=1, source_target_pairs={{0,16},{16,0},{1,17},{17,1},{2,18},{18,2},{3,19},{19,3},{4,20},{20... | collective-permute-start | bytes 98312 | tf_op jit(solution)/shard_map/ppermute | solution.py:225

commit v3 on v2

--- a/solution.py
+++ b/solution.py
@@ -7,6 +7,7 @@
 from jax.experimental import pallas as pl
 from jax.experimental.pallas import tpu as pltpu
 from jax.sharding import PartitionSpec as P
+
 
 HEAD_DIM = 128
 BLOCK = 32
@@ -51,6 +52,7 @@
     columns = offset + jnp.arange(logits.shape[1], dtype=jnp.int32)
     hits = columns[None, :] == wanted[:, None]
     return jnp.sum(jnp.where(hits, logits, 0.0), 1)
+
 
 DIRECT = 4
 SPREAD = 64
@@ -193,8 +195,8 @@
     qcount = queries.shape[1]
     skip = keys.shape[1] // qcount
     rollouts, scored = targets.shape
-    attention = attend_whole if direct("seq") else attend_segments
-    attended = attention(
+    attending = attend_whole if direct("seq") else attend_segments
+    attended = attending(
         queries[0], keys[0], values[0], key_position, compress_keys, compress_values, skip
     )
     part = jnp.dot(attended, out_proj, preferred_element_type=jnp.float32)
@@ -233,6 +235,10 @@
         for i in range(count)
     ]
     return lax.ppermute(block, ("seq", axis), route)
+
+
+def crossed_all(block, axis):
+    return [crossed(block, axis, d) for d in range(lax.axis_size(axis) - 1, 0, -1)][::-1]
 
 
 def compress_all(rows, position, weight):
@@ -260,7 +266,6 @@
 
 
 def attention_kernel(
-    skip,
     k_mine,
     k_other,
     v_mine,
@@ -270,9 +275,8 @@
     position,
     weight_k,
     weight_v,
-    out_proj,
-    base,
-    part,
+    visible,
+    out,
     k_rows,
     v_rows,
     q_rows,
@@ -297,10 +301,7 @@
     keys = compress_all(k_rows, position, weight_k)
     values = compress_all(v_rows, position, weight_v)
     group = q_rows.shape[1] // HEAD_DIM // heads
-    blocks = keys[0].shape[0]
-    row = lax.broadcasted_iota(jnp.int32, (group * count, blocks), 0)
-    column = lax.broadcasted_iota(jnp.int32, (group * count, blocks), 1)
-    visible = column <= row % count * skip // STRIDE
+    seen = visible[...].reshape(group * count, visible.shape[2]) > 0.0
     lanes = []
     for head in range(heads):
         query = jnp.concatenate(
@@ -311,52 +312,56 @@
             0,
         ).astype(jnp.bfloat16)
         scores = lax.dot_general(query, keys[head], NT, preferred_element_type=jnp.float32)
-        scores = jnp.where(visible, scores * (1.0 / math.sqrt(HEAD_DIM)), -1e30)
+        scores = jnp.where(seen, scores * (1.0 / math.sqrt(HEAD_DIM)), -1e30)
         peak = jnp.max(scores, -1, keepdims=True)
-        weights = jnp.where(visible, jnp.exp(scores - peak), 0.0)
+        weights = jnp.where(seen, jnp.exp(scores - peak), 0.0)
         probs = (weights / jnp.sum(weights, -1, keepdims=True)).astype(jnp.bfloat16)
         attended = jnp.dot(probs, values[head], preferred_element_type=jnp.float32)
         attended = attended.astype(jnp.bfloat16).astype(jnp.float32)
         lanes += [attended[g * count : (g + 1) * count, :] for g in range(group)]
-    attended = jnp.concatenate(lanes, 1).astype(jnp.bfloat16)
-    product = jnp.dot(attended, out_proj[...], preferred_element_type=jnp.float32)
-    part[...] = product + base[...]
-
-
-def residual_kernel(residual, base):
+    out[...] = jnp.concatenate(lanes, 1).astype(jnp.bfloat16)
+
+
+def product_kernel(attended, out_proj, residual, part):
     mine = residual[lax.axis_index("batch")].astype(jnp.float32)
-    base[...] = jnp.where(lax.axis_index("mp") == 0, mine, 0.0)
-
-
-def residual_once(residual):
+    part[...] = jnp.where(lax.axis_index("mp") == 0, mine, 0.0) + jnp.dot(
+        attended[...], out_proj[...], preferred_element_type=jnp.float32
+    )
+
+
+def visible_kernel(skip, visible):
+    row = lax.broadcasted_iota(jnp.int32, visible.shape, 1)
+    block = lax.broadcasted_iota(jnp.int32, visible.shape, 2)
+    visible[...] = (block <= row * skip // STRIDE).astype(jnp.float32)
+
+
+def visible_blocks(group, count, blocks, skip):
     return pl.pallas_call(
-        residual_kernel,
-        out_shape=jax.ShapeDtypeStruct(residual.shape[1:], jnp.float32),
-        in_specs=[VMEM],
+        functools.partial(visible_kernel, skip),
+        out_shape=jax.ShapeDtypeStruct((group, count, blocks), jnp.float32),
         out_specs=VMEM,
         compiler_params=pltpu.CompilerParams(vmem_limit_bytes=4 << 20),
-        cost_estimate=pl.CostEstimate(flops=FILL, bytes_accessed=2 * residual.size, transcendentals=0),
-        name="residual",
-    )(residual)
-
-
-def attention_part(
-    keys, values, queries, key_position, compress_keys, compress_values, out_proj, residual, skip
-):
+        cost_estimate=pl.CostEstimate(flops=FILL, bytes_accessed=0, transcendentals=0),
+        name="visible",
+    )()
+
+
+def attention(keys, values, queries, key_position, compress_keys, compress_values, skip):
     length, width = keys.shape
     heads = width // HEAD_DIM
     count = 2 * queries.shape[0]
+    group = queries.shape[1] // HEAD_DIM // heads
     rows = pltpu.VMEM((heads, 2 * length + STRIDE, HEAD_DIM), jnp.float32)
     return pl.pallas_call(
-        functools.partial(attention_kernel, skip),
-        out_shape=jax.ShapeDtypeStruct((count, out_proj.shape[1]), jnp.float32),
-        in_specs=[VMEM] * 11,
+        attention_kernel,
+        out_shape=jax.ShapeDtypeStruct((count, queries.shape[1]), jnp.bfloat16),
+        in_specs=[VMEM] * 10,
         out_specs=VMEM,
         scratch_shapes=[rows, rows, pltpu.VMEM((count, queries.shape[1]), jnp.float32)],
-        compiler_params=pltpu.CompilerParams(vmem_limit_bytes=24 << 20),
+        compiler_params=pltpu.CompilerParams(vmem_limit_bytes=16 << 20),
         cost_estimate=pl.CostEstimate(
-            flops=2 * count * out_proj.size + 8 * length * width * HEAD_DIM * 2,
-            bytes_accessed=2 * (out_proj.size + compress_keys.size + compress_values.size),
+            flops=16 * length * width * HEAD_DIM,
+            bytes_accessed=2 * (compress_keys.size + compress_values.size),
             transcendentals=count * 1024,
         ),
         name="attention",
@@ -370,14 +375,29 @@
         key_position,
         compress_keys,
         compress_values,
-        out_proj,
-        residual_once(residual),
-    )
-
-
-def logits_kernel(batch, *refs):
+        visible_blocks(group, count, 2 * length // STRIDE, skip),
+    )
+
+
+def product(attended, out_proj, residual):
+    return pl.pallas_call(
+        product_kernel,
+        out_shape=jax.ShapeDtypeStruct(residual.shape[1:], jnp.float32),
+        in_specs=[VMEM] * 3,
+        out_specs=VMEM,
+        compiler_params=pltpu.CompilerParams(vmem_limit_bytes=16 << 20),
+        cost_estimate=pl.CostEstimate(
+            flops=2 * attended.shape[0] * out_proj.size,
+            bytes_accessed=2 * out_proj.size,
+            transcendentals=0,
+        ),
+        name="product",
+    )(attended, out_proj, residual)
+
+
+def logits_kernel(batch, scored, skip, *refs):
     near, far = refs[:batch], refs[batch : 2 * batch]
-    gain, lm_head, wanted, sent = refs[2 * batch :]
+    gain, lm_head, facts, sent = refs[2 * batch :]
     core = lax.axis_index("seq")
     blocks = []
     for n, f in zip(near, far):
@@ -395,9 +415,13 @@
     ids = offset + lax.broadcasted_iota(jnp.int32, (share, rows), 0)
     top = jnp.max(logits, 0, keepdims=True)
     total = jnp.sum(jnp.exp(logits - top), 0, keepdims=True)
-    picked = jnp.sum(jnp.where(ids == wanted[...], logits, 0.0), 0, keepdims=True)
-    pad = jnp.zeros((1, sent.shape[1] - 3 * rows), jnp.float32)
-    sent[...] = jnp.broadcast_to(jnp.concatenate([top, total, picked, pad], 1), sent.shape)
+    picked = jnp.sum(jnp.where(ids == facts[0:1, :], logits, 0.0), 0, keepdims=True)
+    spots = lax.broadcasted_iota(jnp.int32, (1, rows), 1) % scored * skip + BLOCK - 1
+    valid = (spots < facts[1:2, :]).astype(jnp.float32)
+    known = [top, total, picked, valid]
+    if sent.shape[1] > 4 * rows:
+        known.append(jnp.zeros((1, sent.shape[1] - 4 * rows), jnp.float32))
+    sent[...] = jnp.broadcast_to(jnp.concatenate(known, 1), sent.shape)
 
 
 def device_index():
@@ -407,42 +431,37 @@
     return index
 
 
-def share_statistics(near, far, norm_gain, lm_head, wanted):
-    rows = wanted.shape[1]
-    across = -(-3 * rows // LANES) * LANES
+def share_statistics(near, far, norm_gain, lm_head, targets, lengths, skip):
+    scored = targets.shape[1]
+    facts = jnp.stack([targets.reshape(-1), jnp.repeat(lengths, scored)], 0)
+    rows = facts.shape[1]
+    across = -(-4 * rows // LANES) * LANES
     return pl.pallas_call(
-        functools.partial(logits_kernel, len(near)),
+        functools.partial(logits_kernel, len(near), scored, skip),
         out_shape=jax.ShapeDtypeStruct((lax.axis_size(EVERY), across), jnp.float32),
         in_specs=[VMEM] * (2 * len(near) + 3),
         out_specs=VMEM,
-        compiler_params=pltpu.CompilerParams(vmem_limit_bytes=24 << 20),
+        compiler_params=pltpu.CompilerParams(vmem_limit_bytes=16 << 20),
         cost_estimate=pl.CostEstimate(
             flops=2 * rows * lm_head.size, bytes_accessed=2 * lm_head.size, transcendentals=rows * 1024
         ),
         name="statistics",
-    )(*near, *far, norm_gain.reshape(1, -1), lm_head, wanted)
-
-
-def score_kernel(skip, scored, few, got, lengths, token, score):
-    rows = lengths.shape[0] * scored
+    )(*near, *far, norm_gain.reshape(1, -1), lm_head, facts)
+
+
+def score_kernel(rows, scored, few, got, token, score):
     tops = got[:, :rows]
     top = jnp.max(tops, 0, keepdims=True)
     total = jnp.sum(got[:, rows : 2 * rows] * jnp.exp(tops - top), 0, keepdims=True)
     picked = jnp.sum(got[:, 2 * rows : 3 * rows], 0, keepdims=True)
     logprob = picked - (top + jnp.log(total))
     index = lax.broadcasted_iota(jnp.int32, (1, rows), 1)
-    spot = index % scored * skip + BLOCK - 1
-    reach = jnp.zeros((1, rows), jnp.int32)
-    for rollout in range(lengths.shape[0]):
-        reach = jnp.where(index // scored == rollout, lengths[rollout], reach)
-    valid = (spot < reach).astype(jnp.float32)
+    valid = got[0:1, 3 * rows : 4 * rows]
     count = jnp.sum(valid, 1, keepdims=True)
     batch = lax.axis_index("batch")
     mine = jnp.where(index // scored == batch, valid * logprob, 0.0)
     score[...] = jnp.sum(mine, 1, keepdims=True) / count
     start = batch * scored + lax.axis_index("seq") * few
-    row = lax.broadcasted_iota(jnp.int32, (rows, few), 0)
-    column = lax.broadcasted_iota(jnp.int32, (rows, few), 1)
     out = jnp.zeros((1, few), jnp.float32)
     lane = lax.broadcasted_iota(jnp.int32, (1, few), 1)
     for j in range(few):
@@ -451,17 +470,18 @@
     token[...] = out
 
 
-def final_scores(got, lengths, scored, few, skip):
+def final_scores(got, rows, scored, few):
     token, score = pl.pallas_call(
-        functools.partial(score_kernel, skip, scored, few),
+        functools.partial(score_kernel, rows, scored, few),
         out_shape=(
             jax.ShapeDtypeStruct((1, few), jnp.float32),
             jax.ShapeDtypeStruct((1, 1), jnp.float32),
         ),
-        in_specs=[VMEM, SMEM],
+        in_specs=[VMEM],
         out_specs=(VMEM, VMEM),
+        compiler_params=pltpu.CompilerParams(vmem_limit_bytes=4 << 20),
         name="scores",
-    )(got, lengths)
+    )(got)
     return token, score.reshape(1)
 
 
@@ -481,25 +501,18 @@
 ):
     few = queries.shape[1]
     skip = keys.shape[1] // few
-    part = attention_part(
-        keys[0],
-        values[0],
-        queries[0],
-        key_position,
-        compress_keys,
-        compress_values,
-        out_proj,
-        residual,
-        skip,
-    )
-    parts = [swap(part)] + [crossed(part, "mp", d) for d in range(1, lax.axis_size("mp"))]
+    attended = attention(
+        keys[0], values[0], queries[0], key_position, compress_keys, compress_values, skip
+    )
+    part = product(attended, out_proj, residual)
+    parts = [swap(part)] + crossed_all(part, "mp")
     far = [pair_sum(parts).astype(jnp.bfloat16)]
-    near = [crossed(far[0], "batch", d) for d in range(1, lax.axis_size("batch"))]
+    near = crossed_all(far[0], "batch")
     far += [swap(block) for block in near]
     near = [swap(far[0])] + near
-    sent = share_statistics(near, far, norm_gain, lm_head, targets.reshape(1, -1))
+    sent = share_statistics(near, far, norm_gain, lm_head, targets, lengths, skip)
     got = lax.all_to_all(sent, EVERY, 0, 0, tiled=True)
-    return final_scores(got, lengths, targets.shape[1], few, skip)
+    return final_scores(got, targets.size, targets.shape[1], few)
 
 
 def body(*arrays):

time: 37.7 us -> 35.4 us (0.939)
  local copies, waits for them, and re-layouts: 2.37 us -> 0.57 us
  waiting for transfers between devices: 9.72 us -> 10.7 us
  Pallas kernels: 4.58 us -> 3.87 us
  blocking collectives: 9.4 us -> 8.86 us
    unnamed x22 -> x24, local copies, waits for them, and re-layouts: 2.29 us -> 0.33 us
    ppermute x8, waiting for transfers between devices: 0.78 us -> 1.83 us  [swap(): return lax.ppermute(block, 'seq', [(0, 1), (1, 0)])]
    pallas_call x4 -> x5, Pallas kernels: 4.58 us -> 3.87 us  [the longest x1 1.2 us: attention(): pl.pallas_call(attention_kernel, out_shape=jax.ShapeDtypeStruct((count, q...]
    all_to_all x1, blocking collectives: 9.4 us -> 8.86 us  [small_mesh(): got = lax.all_to_all(sent, EVERY, 0, 0, tiled=True)]
  transfers between devices with their start and end apart: 14 -> 14, of which waited for: 6 -> 7; matrix products, arithmetic and copies ran while one was open for 0% -> 1% of each run, Pallas kernels for 0% -> 0%
where the time goes in v3:
time: 35.4 us; the launch traced here: 35.3 us
  waiting for transfers between devices  10.7 us (30%)
  starting transfers between devices  10.5 us (30%)
  blocking collectives  8.86 us (25%)
  Pallas kernels  3.87 us (11%)
  between operations  0.78 us (2%)
  local copies, waits for them, and re-layouts  0.57 us (2%)
    ppermute x6, waiting for transfers between devices, crossed(): return lax.ppermute(block, ('seq', axis), route)  8.87 us
    all_to_all x1, blocking collectives, small_mesh(): got = lax.all_to_all(sent, EVERY, 0, 0, tiled=True)  8.86 us
    ppermute x6, starting transfers between devices, crossed(): return lax.ppermute(block, ('seq', axis), route)  8.01 us
    ppermute x8, starting transfers between devices, swap(): return lax.ppermute(block, 'seq', [(0, 1), (1, 0)])  2.45 us
    ppermute x8, waiting for transfers between devices, swap(): return lax.ppermute(block, 'seq', [(0, 1), (1, 0)])  1.83 us
    pallas_call x1, Pallas kernels, attention(): pl.pallas_call(attention_kernel, out_shape=jax.ShapeDtypeStruct((count, q...  1.2 us
    pallas_call x1, Pallas kernels, share_statistics(): pl.pallas_call(functools.partial(logits_kernel, len(near), scored, skip),...  1.03 us
    pallas_call x1, Pallas kernels, final_scores(): pl.pallas_call(functools.partial(score_kernel, rows, scored, few), out_sh...  0.97 us
  transfers between devices with their start and end apart: 14, of which 7 were waited for; matrix products, arithmetic and copies ran while one was open for 1% of the time, Pallas kernels for 0%

profile of v3, /device:TPU:0, one launch (start us, length us, event | category | flops | bytes accessed | tf_op | source)
XLA Modules:
  0.0 35.3 jit_solution(14201225394118063971)
XLA Ops:
  0.6 0.6 %collective-permute-start = (bf16[256,256]{1,0:T(8,128)(2,1)}, bf16[256,256]{1,0:T(8,128)(2,1)S(1)}, u32[]{:S(2)}, u32[]{:S(2)}) collective-permute-start(bf16[256,256]{1,0:T(8,128)(2,1)} %bitcast.9), channel_id=1, source_target_pairs={{0,16},{16,0},{1,17},{17,1},{2,18},{18,2},{3,19},{19,3},{4,20},{20... | collective-permute-start | bytes 393224 | tf_op jit(solution)/shard_map/ppermute | solution.py:227
  1.2 0.1 collective-permute-start.1
  1.3 0.0 copy-start.2
  1.3 0.0 copy-start.3
  1.3 0.0 copy-start.5
  1.3 0.0 copy-start.6
  1.3 0.0 copy-start.7
  1.3 0.0 copy-start.9
  1.3 0.0 copy-start.4
  1.3 0.5 %collective-permute-start.2 = (bf16[4,1024]{1,0:T(4,128)(2,1)}, bf16[4,1024]{1,0:T(4,128)(2,1)S(1)}, u32[]{:S(2)}, u32[]{:S(2)}) collective-permute-start(bf16[4,1024]{1,0:T(4,128)(2,1)} %bitcast.16), channel_id=1, source_target_pairs={{0,16},{16,0},{1,17},{17,1},{2,18},{18,2},{3,19},{19,3},{4,20},{20... | collective-permute-start | bytes 24584 | tf_op jit(solution)/shard_map/ppermute | solution.py:227
  1.8 0.0 copy-start
  1.8 0.0 copy-start.11
  1.8 0.0 copy-start.10
  1.8 0.0 copy-start.1
  1.9 0.0 copy-start.8
  1.9 1.0 %collective-permute-done.2.q_other = bf16[4,1024]{1,0:T(4,128)(2,1)S(1)} collective-permute-done((bf16[4,1024]{1,0:T(4,128)(2,1)}, bf16[4,1024]{1,0:T(4,128)(2,1)S(1)}, u32[]{:S(2)}, u32[]{:S(2)}) %collective-permute-start.2) | collective-permute-done | bytes 8224 | tf_op jit(solution)/shard_map/ppermute | solution.py:227
  2.8 0.0 collective-permute-done.k_other
  2.9 0.0 collective-permute-done.1.v_other
  2.9 0.0 copy-done.2
  2.9 0.0 copy-done.3
  2.9 0.0 copy-done.5
  2.9 0.0 copy-done.6
  2.9 0.0 copy-done.7
  2.9 0.0 copy-done.9
  2.9 1.2 %attention.1.attended = bf16[8,1024]{1,0:T(8,128)(2,1)S(1)} custom-call(bf16[256,256]{1,0:T(8,128)(2,1)S(1)} %bitcast.10, bf16[256,256]{1,0:T(8,128)(2,1)S(1)} %collective-permute-done.k_other, bf16[256,256]{1,0:T(8,128)(2,1)S(1)} %bitcast.12, bf16[256,256]{1,0:T(8,128)(2,1)S(1)} %collective-permute-done.1.v_other, bf16[4,1024]{1,0:T(4,128)(2,1)S(1)} %bitcast.17, ...), custom_call_target="tpu_custom_call" | custom-call | flops 134217728 | bytes 2097152 | tf_op jit(solution)/shard_map/attention/pallas_call | solution.py:355
  4.1 0.0 copy-done.4
  4.1 0.3 copy-done
  4.4 0.7 %product.1 = f32[8,2048]{1,0:T(8,128)S(1)} custom-call(bf16[8,1024]{1,0:T(8,128)(2,1)S(1)} %attention.1.attended, bf16[1024,2048]{1,0:T(8,128)(2,1)S(1)} %copy-done, bf16[4,8,2048]{2,1,0:T(8,128)(2,1)S(1)} %copy-done.4), custom_call_target="tpu_custom_call" | custom-call | flops 33554432 | bytes 4194304 | tf_op jit(solution)/shard_map/product/pallas_call | solution.py:383
  5.1 0.4 %collective-permute-start.3 = (f32[8,2048]{1,0:T(8,128)S(1)}, f32[8,2048]{1,0:T(8,128)S(1)}, u32[]{:S(2)}, u32[]{:S(2)}) collective-permute-start(f32[8,2048]{1,0:T(8,128)S(1)} %product.1), channel_id=1, source_target_pairs={{0,16},{16,0},{1,17},{17,1},{2,18},{18,2},{3,19},{19,3},{4,20},{20... | collective-permute-start | bytes 196616 | tf_op jit(solution)/shard_map/ppermute | solution.py:227
  5.4 2.6 %collective-permute-start.4 = (f32[8,2048]{1,0:T(8,128)S(1)}, f32[8,2048]{1,0:T(8,128)S(1)}, u32[]{:S(2)}, u32[]{:S(2)}) collective-permute-start(f32[8,2048]{1,0:T(8,128)S(1)} %product.1), channel_id=1, source_target_pairs={{0,20},{4,16},{8,28},{12,24},{16,4},{20,0},{24,12},{28,8},{1,21},{... | collective-permute-start | bytes 196616 | tf_op jit(solution)/shard_map/ppermute | solution.py:237
  8.0 1.3 %collective-permute-start.5 = (f32[8,2048]{1,0:T(8,128)S(1)}, f32[8,2048]{1,0:T(8,128)S(1)}, u32[]{:S(2)}, u32[]{:S(2)}) collective-permute-start(f32[8,2048]{1,0:T(8,128)S(1)} %product.1), channel_id=1, source_target_pairs={{0,24},{4,28},{8,16},{12,20},{16,8},{20,12},{24,0},{28,4},{1,25},{... | collective-permute-start | bytes 196616 | tf_op jit(solution)/shard_map/ppermute | solution.py:237
  9.3 0.0 collective-permute-start.6
  9.3 0.0 collective-permute-done.3
  9.3 1.0 %collective-permute-done.4 = f32[8,2048]{1,0:T(8,128)S(1)} collective-permute-done((f32[8,2048]{1,0:T(8,128)S(1)}, f32[8,2048]{1,0:T(8,128)S(1)}, u32[]{:S(2)}, u32[]{:S(2)}) %collective-permute-start.4) | collective-permute-done | bytes 65568 | tf_op jit(solution)/shard_map/ppermute | solution.py:237
  10.3 1.7 %collective-permute-done.5 = f32[8,2048]{1,0:T(8,128)S(1)} collective-permute-done((f32[8,2048]{1,0:T(8,128)S(1)}, f32[8,2048]{1,0:T(8,128)S(1)}, u32[]{:S(2)}, u32[]{:S(2)}) %collective-permute-start.5) | collective-permute-done | bytes 65568 | tf_op jit(solution)/shard_map/ppermute | solution.py:237
  12.0 2.0 %collective-permute-done.6 = f32[8,2048]{1,0:T(8,128)S(1)} collective-permute-done((f32[8,2048]{1,0:T(8,128)S(1)}, f32[8,2048]{1,0:T(8,128)S(1)}, u32[]{:S(2)}, u32[]{:S(2)}) %collective-permute-start.6) | collective-permute-done | bytes 65568 | tf_op jit(solution)/shard_map/ppermute | solution.py:237
  14.1 1.6 %collective-permute-start.8 = (bf16[8,2048]{1,0:T(8,128)(2,1)S(1)}, bf16[8,2048]{1,0:T(8,128)(2,1)S(1)}, u32[]{:S(2)}, u32[]{:S(2)}) collective-permute-start(bf16[8,2048]{1,0:T(8,128)(2,1)S(1)} %add_convert_fusion.refs_4_), channel_id=1, source_target_pairs={{0,17},{1,16},{2,19},{3,18},{16,1},{17,0},{18,3},{19,2},{4,21},{5,... | collective-permute-start | bytes 98312 | tf_op jit(solution)/shard_map/ppermute | solution.py:237
  15.7 2.4 %collective-permute-start.9 = (bf16[8,2048]{1,0:T(8,128)(2,1)S(1)}, bf16[8,2048]{1,0:T(8,128)(2,1)S(1)}, u32[]{:S(2)}, u32[]{:S(2)}) collective-permute-start(bf16[8,2048]{1,0:T(8,128)(2,1)S(1)} %add_convert_fusion.refs_4_), channel_id=1, source_target_pairs={{0,18},{1,19},{2,16},{3,17},{16,2},{17,3},{18,0},{19,1},{4,22},{5,... | collective-permute-start | bytes 98312 | tf_op jit(solution)/shard_map/ppermute | solution.py:237
  18.1 0.2 collective-permute-start.10
  18.2 0.0 copy-done.11
  18.2 0.1 broadcast_in_dim.3
  18.3 0.1 stack_reshape.7
  18.4 0.0 copy-done.10
  18.4 0.1 stack_reshape.6
  18.5 0.2 collective-permute-start.7
  18.6 0.0 collective-permute-done.8.refs_1_
  18.6 0.3 collective-permute-start.11
  19.0 1.8 %collective-permute-done.9.refs_2_ = bf16[8,2048]{1,0:T(8,128)(2,1)S(1)} collective-permute-done((bf16[8,2048]{1,0:T(8,128)(2,1)S(1)}, bf16[8,2048]{1,0:T(8,128)(2,1)S(1)}, u32[]{:S(2)}, u32[]{:S(2)}) %collective-permute-start.9) | collective-permute-done | bytes 32800 | tf_op jit(solution)/shard_map/ppermute | solution.py:237
  20.8 0.1 collective-permute-start.12
  20.9 2.3 %collective-permute-done.10.refs_3_ = bf16[8,2048]{1,0:T(8,128)(2,1)S(1)} collective-permute-done((bf16[8,2048]{1,0:T(8,128)(2,1)S(1)}, bf16[8,2048]{1,0:T(8,128)(2,1)S(1)}, u32[]{:S(2)}, u32[]{:S(2)}) %collective-permute-start.10) | collective-permute-done | bytes 32800 | tf_op jit(solution)/shard_map/ppermute | solution.py:237
  23.2 0.3 collective-permute-start.13
  23.5 0.0 collective-permute-done.7.refs_0_
  23.5 0.0 collective-permute-done.11.refs_5_
  23.6 0.0 collective-permute-done.12.refs_6_
  23.6 0.8 %collective-permute-done.13.refs_7_ = bf16[8,2048]{1,0:T(8,128)(2,1)S(1)} collective-permute-done((bf16[8,2048]{1,0:T(8,128)(2,1)S(1)}, bf16[8,2048]{1,0:T(8,128)(2,1)S(1)}, u32[]{:S(2)}, u32[]{:S(2)}) %collective-permute-start.13) | collective-permute-done | bytes 32800 | tf_op jit(solution)/shard_map/ppermute | solution.py:227
  24.4 0.0 copy-done.1
  24.4 0.0 copy-done.8
  24.4 1.0 %statistics.1 = f32[32,128]{1,0:T(8,128)S(1)} custom-call(bf16[8,2048]{1,0:T(8,128)(2,1)S(1)} %collective-permute-done.7.refs_0_, bf16[8,2048]{1,0:T(8,128)(2,1)S(1)} %collective-permute-done.8.refs_1_, bf16[8,2048]{1,0:T(8,128)(2,1)S(1)} %collective-permute-done.9.refs_2_, bf16[8,2048]{1,0:T(8,128)(2,1)S(1)} %collective-permute-done.10.refs_3_, ...), custom_call_target="tpu_custom_call" | custom-call | flops 67108864 | bytes 2097152 | tf_op jit(solution)/shard_map/statistics/pallas_call | solution.py:439
  25.4 8.9 %all_to_all.11 = f32[32,1,128]{2,1,0:T(1,128)S(1)} all-to-all(f32[32,1,128]{2,1,0:T(1,128)S(1)} %bitcast.13), channel_id=1, replica_groups=mesh['seq'=2,'mp'=4,'batch'=4] {'seq','mp','batch'}, dimensions={0} | all-to-all | bytes 32768 | tf_op jit(solution)/shard_map/all_to_all | solution.py:514
  34.3 1.0 %scores.1 = (f32[1,4]{1,0:T(1,128)}, f32[1,1]{1,0:T(1,128)}) custom-call(f32[32,128]{1,0:T(8,128)S(1)} %bitcast.14), custom_call_target="tpu_custom_call" | custom-call | tf_op jit(solution)/shard_map/scores/pallas_call | solution.py:474
  (3 shorter events, 0.0 us)
Async XLA Ops:
  0.6 2.2 %collective-permute-start = (bf16[256,256]{1,0:T(8,128)(2,1)}, bf16[256,256]{1,0:T(8,128)(2,1)S(1)}, u32[]{:S(2)}, u32[]{:S(2)}) collective-permute-start(bf16[256,256]{1,0:T(8,128)(2,1)} %bitcast.9), channel_id=1, source_target_pairs={{0,16},{16,0},{1,17},{17,1},{2,18},{18,2},{3,19},{19,3},{4,20},{20... | collective-permute-start | bytes 393224 | tf_op jit(solution)/shard_map/ppermute | solution.py:227
  1.2 1.7 %collective-permute-start.1 = (bf16[256,256]{1,0:T(8,128)(2,1)}, bf16[256,256]{1,0:T(8,128)(2,1)S(1)}, u32[]{:S(2)}, u32[]{:S(2)}) collective-permute-start(bf16[256,256]{1,0:T(8,128)(2,1)} %bitcast.11), channel_id=1, source_target_pairs={{0,16},{16,0},{1,17},{17,1},{2,18},{18,2},{3,19},{19,3},{4,20},{20... | collective-permute-start | bytes 393224 | tf_op jit(solution)/shard_map/ppermute | solution.py:227
  1.3 1.6 %copy-start.2 = (bf16[4096,128]{1,0:T(8,128)(2,1)S(1)}, bf16[4096,128]{1,0:T(8,128)(2,1)}, u32[]{:S(2)}) copy-start(bf16[4096,128]{1,0:T(8,128)(2,1)} %weight_k.1) | copy-start | bytes 3145732
  1.3 1.6 %copy-start.3 = (bf16[4096,128]{1,0:T(8,128)(2,1)S(1)}, bf16[4096,128]{1,0:T(8,128)(2,1)}, u32[]{:S(2)}) copy-start(bf16[4096,128]{1,0:T(8,128)(2,1)} %weight_v.1) | copy-start | bytes 3145732
  1.3 1.6 %copy-start.5 = (bf16[1,256,256]{2,1,0:T(8,128)(2,1)S(1)}, bf16[1,256,256]{2,1,0:T(8,128)(2,1)}, u32[]{:S(2)}) copy-start(bf16[1,256,256]{2,1,0:T(8,128)(2,1)} %param.13) | copy-start | bytes 393220
  1.3 1.6 %copy-start.6 = (bf16[1,256,256]{2,1,0:T(8,128)(2,1)S(1)}, bf16[1,256,256]{2,1,0:T(8,128)(2,1)}, u32[]{:S(2)}) copy-start(bf16[1,256,256]{2,1,0:T(8,128)(2,1)} %param.14) | copy-start | bytes 393220
  1.3 1.6 %copy-start.7 = (f32[32,128]{1,0:T(8,128)S(1)}, f32[32,128]{1,0:T(8,128)}, u32[]{:S(2)}) copy-start(f32[32,128]{1,0:T(8,128)} %position.1) | copy-start | bytes 49156
  1.3 1.6 %copy-start.9 = (bf16[1,4,1024]{2,1,0:T(4,128)(2,1)S(1)}, bf16[1,4,1024]{2,1,0:T(4,128)(2,1)}, u32[]{:S(2)}) copy-start(bf16[1,4,1024]{2,1,0:T(4,128)(2,1)} %param.12) | copy-start | bytes 24580
  1.3 2.8 %copy-start.4 = (bf16[4,8,2048]{2,1,0:T(8,128)(2,1)S(1)}, bf16[4,8,2048]{2,1,0:T(8,128)(2,1)}, u32[]{:S(2)}) copy-start(bf16[4,8,2048]{2,1,0:T(8,128)(2,1)} %residual.1) | copy-start | bytes 393220
  1.3 1.5 %collective-permute-start.2 = (bf16[4,1024]{1,0:T(4,128)(2,1)}, bf16[4,1024]{1,0:T(4,128)(2,1)S(1)}, u32[]{:S(2)}, u32[]{:S(2)}) collective-permute-start(bf16[4,1024]{1,0:T(4,128)(2,1)} %bitcast.16), channel_id=1, source_target_pairs={{0,16},{16,0},{1,17},{17,1},{2,18},{18,2},{3,19},{19,3},{4,20},{20... | collective-permute-start | bytes 24584 | tf_op jit(solution)/shard_map/ppermute | solution.py:227
  1.8 2.6 %copy-start = (bf16[1024,2048]{1,0:T(8,128)(2,1)S(1)}, bf16[1024,2048]{1,0:T(8,128)(2,1)}, u32[]{:S(2)}) copy-start(bf16[1024,2048]{1,0:T(8,128)(2,1)} %out_proj.1) | copy-start | bytes 12582916
  1.8 16.4 %copy-start.11 = (s32[4]{0:T(128)S(1)}, s32[4]{0:T(128)}, u32[]{:S(2)}) copy-start(s32[4]{0:T(128)} %param.23) | copy-start | bytes 52
  1.8 16.5 %copy-start.10 = (s32[4,8]{1,0:T(4,128)S(1)}, s32[4,8]{1,0:T(4,128)}, u32[]{:S(2)}) copy-start(s32[4,8]{1,0:T(4,128)} %param.22) | copy-start | bytes 388
  1.8 22.6 %copy-start.1 = (bf16[256,4096]{1,0:T(8,128)(2,1)S(1)}, bf16[256,4096]{1,0:T(8,128)(2,1)}, u32[]{:S(2)}) copy-start(bf16[256,4096]{1,0:T(8,128)(2,1)} %refs_9_.1) | copy-start | bytes 6291460
  1.9 22.5 %copy-start.8 = (f32[4096]{0:T(1024)S(1)}, f32[4096]{0:T(1024)}, u32[]{:S(2)}) copy-start(f32[4096]{0:T(1024)} %param.20) | copy-start | bytes 49156
  5.1 4.3 %collective-permute-start.3 = (f32[8,2048]{1,0:T(8,128)S(1)}, f32[8,2048]{1,0:T(8,128)S(1)}, u32[]{:S(2)}, u32[]{:S(2)}) collective-permute-start(f32[8,2048]{1,0:T(8,128)S(1)} %product.1), channel_id=1, source_target_pairs={{0,16},{16,0},{1,17},{17,1},{2,18},{18,2},{3,19},{19,3},{4,20},{20... | collective-permute-start | bytes 196616 | tf_op jit(solution)/shard_map/ppermute | solution.py:227
  5.4 4.9 %collective-permute-start.4 = (f32[8,2048]{1,0:T(8,128)S(1)}, f32[8,2048]{1,0:T(8,128)S(1)}, u32[]{:S(2)}, u32[]{:S(2)}) collective-permute-start(f32[8,2048]{1,0:T(8,128)S(1)} %product.1), channel_id=1, source_target_pairs={{0,20},{4,16},{8,28},{12,24},{16,4},{20,0},{24,12},{28,8},{1,21},{... | collective-permute-start | bytes 196616 | tf_op jit(solution)/shard_map/ppermute | solution.py:237
  8.0 4.0 %collective-permute-start.5 = (f32[8,2048]{1,0:T(8,128)S(1)}, f32[8,2048]{1,0:T(8,128)S(1)}, u32[]{:S(2)}, u32[]{:S(2)}) collective-permute-start(f32[8,2048]{1,0:T(8,128)S(1)} %product.1), channel_id=1, source_target_pairs={{0,24},{4,28},{8,16},{12,20},{16,8},{20,12},{24,0},{28,4},{1,25},{... | collective-permute-start | bytes 196616 | tf_op jit(solution)/shard_map/ppermute | solution.py:237
  9.3 4.8 %collective-permute-start.6 = (f32[8,2048]{1,0:T(8,128)S(1)}, f32[8,2048]{1,0:T(8,128)S(1)}, u32[]{:S(2)}, u32[]{:S(2)}) collective-permute-start(f32[8,2048]{1,0:T(8,128)S(1)} %product.1), channel_id=1, source_target_pairs={{0,28},{4,24},{8,20},{12,16},{16,12},{20,8},{24,4},{28,0},{1,29},{... | collective-permute-start | bytes 196616 | tf_op jit(solution)/shard_map/ppermute | solution.py:237
  14.1 4.5 %collective-permute-start.8 = (bf16[8,2048]{1,0:T(8,128)(2,1)S(1)}, bf16[8,2048]{1,0:T(8,128)(2,1)S(1)}, u32[]{:S(2)}, u32[]{:S(2)}) collective-permute-start(bf16[8,2048]{1,0:T(8,128)(2,1)S(1)} %add_convert_fusion.refs_4_), channel_id=1, source_target_pairs={{0,17},{1,16},{2,19},{3,18},{16,1},{17,0},{18,3},{19,2},{4,21},{5,... | collective-permute-start | bytes 98312 | tf_op jit(solution)/shard_map/ppermute | solution.py:237
  15.7 5.1 %collective-permute-start.9 = (bf16[8,2048]{1,0:T(8,128)(2,1)S(1)}, bf16[8,2048]{1,0:T(8,128)(2,1)S(1)}, u32[]{:S(2)}, u32[]{:S(2)}) collective-permute-start(bf16[8,2048]{1,0:T(8,128)(2,1)S(1)} %add_convert_fusion.refs_4_), channel_id=1, source_target_pairs={{0,18},{1,19},{2,16},{3,17},{16,2},{17,3},{18,0},{19,1},{4,22},{5,... | collective-permute-start | bytes 98312 | tf_op jit(solution)/shard_map/ppermute | solution.py:237
  18.1 5.1 %collective-permute-start.10 = (bf16[8,2048]{1,0:T(8,128)(2,1)S(1)}, bf16[8,2048]{1,0:T(8,128)(2,1)S(1)}, u32[]{:S(2)}, u32[]{:S(2)}) collective-permute-start(bf16[8,2048]{1,0:T(8,128)(2,1)S(1)} %add_convert_fusion.refs_4_), channel_id=1, source_target_pairs={{0,19},{1,18},{2,17},{3,16},{16,3},{17,2},{18,1},{19,0},{4,23},{5,... | collective-permute-start | bytes 98312 | tf_op jit(solution)/shard_map/ppermute | solution.py:237
  18.5 5.1 %collective-permute-start.7 = (bf16[8,2048]{1,0:T(8,128)(2,1)S(1)}, bf16[8,2048]{1,0:T(8,128)(2,1)S(1)}, u32[]{:S(2)}, u32[]{:S(2)}) collective-permute-start(bf16[8,2048]{1,0:T(8,128)(2,1)S(1)} %add_convert_fusion.refs_4_), channel_id=1, source_target_pairs={{0,16},{16,0},{1,17},{17,1},{2,18},{18,2},{3,19},{19,3},{4,20},{20... | collective-permute-start | bytes 98312 | tf_op jit(solution)/shard_map/ppermute | solution.py:227
  18.6 4.9 %collective-permute-start.11 = (bf16[8,2048]{1,0:T(8,128)(2,1)S(1)}, bf16[8,2048]{1,0:T(8,128)(2,1)S(1)}, u32[]{:S(2)}, u32[]{:S(2)}) collective-permute-start(bf16[8,2048]{1,0:T(8,128)(2,1)S(1)} %collective-permute-done.8.refs_1_), channel_id=1, source_target_pairs={{0,16},{16,0},{1,17},{17,1},{2,18},{18,2},{3,19},{19,3},{4,20},{20... | collective-permute-start | bytes 98312 | tf_op jit(solution)/shard_map/ppermute | solution.py:227
  20.8 2.7 %collective-permute-start.12 = (bf16[8,2048]{1,0:T(8,128)(2,1)S(1)}, bf16[8,2048]{1,0:T(8,128)(2,1)S(1)}, u32[]{:S(2)}, u32[]{:S(2)}) collective-permute-start(bf16[8,2048]{1,0:T(8,128)(2,1)S(1)} %collective-permute-done.9.refs_2_), channel_id=1, source_target_pairs={{0,16},{16,0},{1,17},{17,1},{2,18},{18,2},{3,19},{19,3},{4,20},{20... | collective-permute-start | bytes 98312 | tf_op jit(solution)/shard_map/ppermute | solution.py:227
  23.2 1.2 %collective-permute-start.13 = (bf16[8,2048]{1,0:T(8,128)(2,1)S(1)}, bf16[8,2048]{1,0:T(8,128)(2,1)S(1)}, u32[]{:S(2)}, u32[]{:S(2)}) collective-permute-start(bf16[8,2048]{1,0:T(8,128)(2,1)S(1)} %collective-permute-done.10.refs_3_), channel_id=1, source_target_pairs={{0,16},{16,0},{1,17},{17,1},{2,18},{18,2},{3,19},{19,3},{4,20},{20... | collective-permute-start | bytes 98312 | tf_op jit(solution)/shard_map/ppermute | solution.py:227

commit v4 on v3

--- a/solution.py
+++ b/solution.py
@@ -395,17 +395,15 @@
     )(attended, out_proj, residual)
 
 
-def logits_kernel(batch, scored, skip, *refs):
-    near, far = refs[:batch], refs[batch : 2 * batch]
-    gain, lm_head, facts, sent = refs[2 * batch :]
+def logits_kernel(scored, skip, *refs):
+    near_mine, near_others, far_mine, far_others, gain, lm_head, facts, sent = refs
     core = lax.axis_index("seq")
     blocks = []
-    for n, f in zip(near, far):
+    for n, f in ((near_mine, far_mine), (near_others, far_others)):
         n = n[...].astype(jnp.float32)
         f = f[...].astype(jnp.float32)
-        blocks.append(
-            jnp.concatenate([jnp.where(core == 0, n, f), jnp.where(core == 0, f, n)], 1)
-        )
+        both = jnp.concatenate([jnp.where(core == 0, n, f), jnp.where(core == 0, f, n)], 1)
+        blocks += [both[r : r + scored] for r in range(0, both.shape[0], scored)]
     hidden = jnp.concatenate(by_position(blocks, "batch"), 0)
     meansq = jnp.mean(hidden * hidden, -1, keepdims=True)
     normed = (hidden * lax.rsqrt(meansq + 1e-05) * gain[...]).astype(jnp.bfloat16)
@@ -437,7 +435,7 @@
     rows = facts.shape[1]
     across = -(-4 * rows // LANES) * LANES
     return pl.pallas_call(
-        functools.partial(logits_kernel, len(near), scored, skip),
+        functools.partial(logits_kernel, scored, skip),
         out_shape=jax.ShapeDtypeStruct((lax.axis_size(EVERY), across), jnp.float32),
         in_specs=[VMEM] * (2 * len(near) + 3),
         out_specs=VMEM,
@@ -462,12 +460,9 @@
     mine = jnp.where(index // scored == batch, valid * logprob, 0.0)
     score[...] = jnp.sum(mine, 1, keepdims=True) / count
     start = batch * scored + lax.axis_index("seq") * few
-    out = jnp.zeros((1, few), jnp.float32)
-    lane = lax.broadcasted_iota(jnp.int32, (1, few), 1)
-    for j in range(few):
-        value = jnp.sum(jnp.where(index == start + j, logprob, 0.0), 1, keepdims=True)
-        out = jnp.where(lane == j, value, out)
-    token[...] = out
+    spare = jnp.zeros((1, got.shape[1] - rows), jnp.float32)
+    turned = pltpu.roll(jnp.concatenate([logprob, spare], 1), got.shape[1] - start, 1)
+    token[...] = turned[:, :few]
 
 
 def final_scores(got, rows, scored, few):
@@ -505,11 +500,12 @@
         keys[0], values[0], queries[0], key_position, compress_keys, compress_values, skip
     )
     part = product(attended, out_proj, residual)
-    parts = [swap(part)] + crossed_all(part, "mp")
+    parts = [swap(part)]
+    parts += crossed_all(part, "mp")
     far = [pair_sum(parts).astype(jnp.bfloat16)]
     near = crossed_all(far[0], "batch")
-    far += [swap(block) for block in near]
-    near = [swap(far[0])] + near
+    near = [swap(far[0]), jnp.concatenate(near, 0)]
+    far.append(swap(near[1]))
     sent = share_statistics(near, far, norm_gain, lm_head, targets, lengths, skip)
     got = lax.all_to_all(sent, EVERY, 0, 0, tiled=True)
     return final_scores(got, targets.size, targets.shape[1], few)

time: 35.4 us -> 35.8 us (1.011)
  waiting for transfers between devices: 10.7 us -> 11.5 us
  starting transfers between devices: 10.5 us -> 10 us
    ppermute x6, waiting for transfers between devices: 8.87 us -> 9.56 us  [crossed(): return lax.ppermute(block, ('seq', axis), route)]
    ppermute x8 -> x6, starting transfers between devices: 2.45 us -> 2 us  [swap(): return lax.ppermute(block, 'seq', [(0, 1), (1, 0)])]
    ppermute x8 -> x6, waiting for transfers between devices: 1.83 us -> 1.94 us  [swap(): return lax.ppermute(block, 'seq', [(0, 1), (1, 0)])]
  transfers between devices with their start and end apart: 14 -> 12, of which waited for: 7 -> 7; matrix products, arithmetic and copies ran while one was open for 1% -> 1% of each run, Pallas kernels for 0% -> 0%
where the time goes in v4:
time: 35.8 us; the launch traced here: 35.6 us
  waiting for transfers between devices  11.5 us (32%)
  starting transfers between devices  10 us (28%)
  blocking collectives  8.86 us (25%)
  Pallas kernels  3.87 us (11%)
  between operations  0.77 us (2%)
  local copies, waits for them, and re-layouts  0.58 us (2%)
    ppermute x6, waiting for transfers between devices, crossed(): return lax.ppermute(block, ('seq', axis), route)  9.56 us
    all_to_all x1, blocking collectives, small_mesh(): got = lax.all_to_all(sent, EVERY, 0, 0, tiled=True)  8.86 us
    ppermute x6, starting transfers between devices, crossed(): return lax.ppermute(block, ('seq', axis), route)  8.01 us
    ppermute x6, starting transfers between devices, swap(): return lax.ppermute(block, 'seq', [(0, 1), (1, 0)])  2 us
    ppermute x6, waiting for transfers between devices, swap(): return lax.ppermute(block, 'seq', [(0, 1), (1, 0)])  1.94 us
    pallas_call x1, Pallas kernels, attention(): pl.pallas_call(attention_kernel, out_shape=jax.ShapeDtypeStruct((count, q...  1.2 us
    pallas_call x1, Pallas kernels, share_statistics(): pl.pallas_call(functools.partial(logits_kernel, scored, skip), out_shape=...  1.03 us
    pallas_call x1, Pallas kernels, final_scores(): pl.pallas_call(functools.partial(score_kernel, rows, scored, few), out_sh...  0.97 us
  transfers between devices with their start and end apart: 12, of which 7 were waited for; matrix products, arithmetic and copies ran while one was open for 1% of the time, Pallas kernels for 0%

profile of v4, /device:TPU:0, one launch (start us, length us, event | category | flops | bytes accessed | tf_op | source)
XLA Modules:
  0.0 35.6 jit_solution(11486129659931430519)
XLA Ops:
  0.6 0.6 %collective-permute-start = (bf16[256,256]{1,0:T(8,128)(2,1)}, bf16[256,256]{1,0:T(8,128)(2,1)S(1)}, u32[]{:S(2)}, u32[]{:S(2)}) collective-permute-start(bf16[256,256]{1,0:T(8,128)(2,1)} %bitcast.9), channel_id=1, source_target_pairs={{0,16},{16,0},{1,17},{17,1},{2,18},{18,2},{3,19},{19,3},{4,20},{20... | collective-permute-start | bytes 393224 | tf_op jit(solution)/shard_map/ppermute | solution.py:227
  1.2 0.1 collective-permute-start.1
  1.3 0.0 copy-start.2
  1.3 0.0 copy-start.3
  1.3 0.0 copy-start.5
  1.3 0.0 copy-start.6
  1.3 0.0 copy-start.7
  1.3 0.0 copy-start.9
  1.3 0.0 copy-start.4
  1.3 0.5 %collective-permute-start.2 = (bf16[4,1024]{1,0:T(4,128)(2,1)}, bf16[4,1024]{1,0:T(4,128)(2,1)S(1)}, u32[]{:S(2)}, u32[]{:S(2)}) collective-permute-start(bf16[4,1024]{1,0:T(4,128)(2,1)} %bitcast.16), channel_id=1, source_target_pairs={{0,16},{16,0},{1,17},{17,1},{2,18},{18,2},{3,19},{19,3},{4,20},{20... | collective-permute-start | bytes 24584 | tf_op jit(solution)/shard_map/ppermute | solution.py:227
  1.8 0.0 copy-start
  1.8 0.0 copy-start.11
  1.8 0.0 copy-start.10
  1.8 0.0 copy-start.1
  1.9 0.0 copy-start.8
  1.9 1.0 %collective-permute-done.2.q_other = bf16[4,1024]{1,0:T(4,128)(2,1)S(1)} collective-permute-done((bf16[4,1024]{1,0:T(4,128)(2,1)}, bf16[4,1024]{1,0:T(4,128)(2,1)S(1)}, u32[]{:S(2)}, u32[]{:S(2)}) %collective-permute-start.2) | collective-permute-done | bytes 8224 | tf_op jit(solution)/shard_map/ppermute | solution.py:227
  2.8 0.0 collective-permute-done.k_other
  2.9 0.0 collective-permute-done.1.v_other
  2.9 0.0 copy-done.2
  2.9 0.0 copy-done.3
  2.9 0.0 copy-done.5
  2.9 0.0 copy-done.6
  2.9 0.0 copy-done.7
  2.9 0.0 copy-done.9
  2.9 1.2 %attention.1.attended = bf16[8,1024]{1,0:T(8,128)(2,1)S(1)} custom-call(bf16[256,256]{1,0:T(8,128)(2,1)S(1)} %bitcast.10, bf16[256,256]{1,0:T(8,128)(2,1)S(1)} %collective-permute-done.k_other, bf16[256,256]{1,0:T(8,128)(2,1)S(1)} %bitcast.12, bf16[256,256]{1,0:T(8,128)(2,1)S(1)} %collective-permute-done.1.v_other, bf16[4,1024]{1,0:T(4,128)(2,1)S(1)} %bitcast.17, ...), custom_call_target="tpu_custom_call" | custom-call | flops 134217728 | bytes 2097152 | tf_op jit(solution)/shard_map/attention/pallas_call | solution.py:355
  4.1 0.0 copy-done.4
  4.1 0.3 copy-done
  4.4 0.7 %product.1 = f32[8,2048]{1,0:T(8,128)S(1)} custom-call(bf16[8,1024]{1,0:T(8,128)(2,1)S(1)} %attention.1.attended, bf16[1024,2048]{1,0:T(8,128)(2,1)S(1)} %copy-done, bf16[4,8,2048]{2,1,0:T(8,128)(2,1)S(1)} %copy-done.4), custom_call_target="tpu_custom_call" | custom-call | flops 33554432 | bytes 4194304 | tf_op jit(solution)/shard_map/product/pallas_call | solution.py:383
  5.1 0.4 collective-permute-start.3
  5.4 2.6 %collective-permute-start.4 = (f32[8,2048]{1,0:T(8,128)S(1)}, f32[8,2048]{1,0:T(8,128)S(1)}, u32[]{:S(2)}, u32[]{:S(2)}) collective-permute-start(f32[8,2048]{1,0:T(8,128)S(1)} %product.1), channel_id=1, source_target_pairs={{0,20},{4,16},{8,28},{12,24},{16,4},{20,0},{24,12},{28,8},{1,21},{... | collective-permute-start | bytes 196616 | tf_op jit(solution)/shard_map/ppermute | solution.py:237
  8.0 1.3 %collective-permute-start.5 = (f32[8,2048]{1,0:T(8,128)S(1)}, f32[8,2048]{1,0:T(8,128)S(1)}, u32[]{:S(2)}, u32[]{:S(2)}) collective-permute-start(f32[8,2048]{1,0:T(8,128)S(1)} %product.1), channel_id=1, source_target_pairs={{0,24},{4,28},{8,16},{12,20},{16,8},{20,12},{24,0},{28,4},{1,25},{... | collective-permute-start | bytes 196616 | tf_op jit(solution)/shard_map/ppermute | solution.py:237
  9.3 0.0 collective-permute-start.6
  9.3 0.0 collective-permute-done.3
  9.3 1.0 %collective-permute-done.4 = f32[8,2048]{1,0:T(8,128)S(1)} collective-permute-done((f32[8,2048]{1,0:T(8,128)S(1)}, f32[8,2048]{1,0:T(8,128)S(1)}, u32[]{:S(2)}, u32[]{:S(2)}) %collective-permute-start.4) | collective-permute-done | bytes 65568 | tf_op jit(solution)/shard_map/ppermute | solution.py:237
  10.3 1.7 %collective-permute-done.5 = f32[8,2048]{1,0:T(8,128)S(1)} collective-permute-done((f32[8,2048]{1,0:T(8,128)S(1)}, f32[8,2048]{1,0:T(8,128)S(1)}, u32[]{:S(2)}, u32[]{:S(2)}) %collective-permute-start.5) | collective-permute-done | bytes 65568 | tf_op jit(solution)/shard_map/ppermute | solution.py:237
  12.0 2.0 %collective-permute-done.6 = f32[8,2048]{1,0:T(8,128)S(1)} collective-permute-done((f32[8,2048]{1,0:T(8,128)S(1)}, f32[8,2048]{1,0:T(8,128)S(1)}, u32[]{:S(2)}, u32[]{:S(2)}) %collective-permute-start.6) | collective-permute-done | bytes 65568 | tf_op jit(solution)/shard_map/ppermute | solution.py:237
  14.1 1.6 %collective-permute-start.8 = (bf16[8,2048]{1,0:T(8,128)(2,1)S(1)}, bf16[8,2048]{1,0:T(8,128)(2,1)S(1)}, u32[]{:S(2)}, u32[]{:S(2)}) collective-permute-start(bf16[8,2048]{1,0:T(8,128)(2,1)S(1)} %add_convert_fusion.refs_2_), channel_id=1, source_target_pairs={{0,17},{1,16},{2,19},{3,18},{16,1},{17,0},{18,3},{19,2},{4,21},{5,... | collective-permute-start | bytes 98312 | tf_op jit(solution)/shard_map/ppermute | solution.py:237
  15.7 0.0 copy-done.11
  15.7 0.1 broadcast_in_dim.3
  15.8 0.1 stack_reshape.7
  15.8 0.0 copy-done.10
  15.8 0.1 stack_reshape.6
  15.9 2.4 %collective-permute-start.9 = (bf16[8,2048]{1,0:T(8,128)(2,1)S(1)}, bf16[8,2048]{1,0:T(8,128)(2,1)S(1)}, u32[]{:S(2)}, u32[]{:S(2)}) collective-permute-start(bf16[8,2048]{1,0:T(8,128)(2,1)S(1)} %add_convert_fusion.refs_2_), channel_id=1, source_target_pairs={{0,18},{1,19},{2,16},{3,17},{16,2},{17,3},{18,0},{19,1},{4,22},{5,... | collective-permute-start | bytes 98312 | tf_op jit(solution)/shard_map/ppermute | solution.py:237
  18.3 0.2 collective-permute-start.10
  18.5 0.2 collective-permute-start.7
  18.6 0.0 collective-permute-done.8
  18.6 2.3 %collective-permute-done.9 = bf16[8,2048]{1,0:T(8,128)(2,1)S(1)} collective-permute-done((bf16[8,2048]{1,0:T(8,128)(2,1)S(1)}, bf16[8,2048]{1,0:T(8,128)(2,1)S(1)}, u32[]{:S(2)}, u32[]{:S(2)}) %collective-permute-start.9) | collective-permute-done | bytes 32800 | tf_op jit(solution)/shard_map/ppermute | solution.py:237
  21.0 2.4 %collective-permute-done.10 = bf16[8,2048]{1,0:T(8,128)(2,1)S(1)} collective-permute-done((bf16[8,2048]{1,0:T(8,128)(2,1)S(1)}, bf16[8,2048]{1,0:T(8,128)(2,1)S(1)}, u32[]{:S(2)}, u32[]{:S(2)}) %collective-permute-start.10) | collective-permute-done | bytes 32800 | tf_op jit(solution)/shard_map/ppermute | solution.py:237
  23.4 0.3 collective-permute-start.11
  23.8 0.0 collective-permute-done.7.refs_0_
  23.8 1.0 %collective-permute-done.11.refs_3_ = bf16[24,2048]{1,0:T(8,128)(2,1)S(1)} collective-permute-done((bf16[24,2048]{1,0:T(8,128)(2,1)S(1)}, bf16[24,2048]{1,0:T(8,128)(2,1)S(1)}, u32[]{:S(2)}, u32[]{:S(2)}) %collective-permute-start.11) | collective-permute-done | bytes 98336 | tf_op jit(solution)/shard_map/ppermute | solution.py:227
  24.7 0.0 copy-done.1
  24.7 0.0 copy-done.8
  24.7 1.0 %statistics.1 = f32[32,128]{1,0:T(8,128)S(1)} custom-call(bf16[8,2048]{1,0:T(8,128)(2,1)S(1)} %collective-permute-done.7.refs_0_, bf16[24,2048]{1,0:T(8,128)(2,1)S(1)} %constant_dynamic-update-slice_fusion.refs_1_, bf16[8,2048]{1,0:T(8,128)(2,1)S(1)} %add_convert_fusion.refs_2_, bf16[24,2048]{1,0:T(8,128)(2,1)S(1)} %collective-permute-done.11.refs_3_, ...), custom_call_target="tpu_custom_call" | custom-call | flops 67108864 | bytes 2097152 | tf_op jit(solution)/shard_map/statistics/pallas_call | solution.py:437
  25.8 8.9 %all_to_all.11 = f32[32,1,128]{2,1,0:T(1,128)S(1)} all-to-all(f32[32,1,128]{2,1,0:T(1,128)S(1)} %bitcast.13), channel_id=1, replica_groups=mesh['seq'=2,'mp'=4,'batch'=4] {'seq','mp','batch'}, dimensions={0} | all-to-all | bytes 32768 | tf_op jit(solution)/shard_map/all_to_all | solution.py:510
  34.6 1.0 %scores.1 = (f32[1,4]{1,0:T(1,128)}, f32[1,1]{1,0:T(1,128)}) custom-call(f32[32,128]{1,0:T(8,128)S(1)} %bitcast.14), custom_call_target="tpu_custom_call" | custom-call | tf_op jit(solution)/shard_map/scores/pallas_call | solution.py:469
  (6 shorter events, 0.0 us)
Async XLA Ops:
  0.6 2.2 %collective-permute-start = (bf16[256,256]{1,0:T(8,128)(2,1)}, bf16[256,256]{1,0:T(8,128)(2,1)S(1)}, u32[]{:S(2)}, u32[]{:S(2)}) collective-permute-start(bf16[256,256]{1,0:T(8,128)(2,1)} %bitcast.9), channel_id=1, source_target_pairs={{0,16},{16,0},{1,17},{17,1},{2,18},{18,2},{3,19},{19,3},{4,20},{20... | collective-permute-start | bytes 393224 | tf_op jit(solution)/shard_map/ppermute | solution.py:227
  1.2 1.7 %collective-permute-start.1 = (bf16[256,256]{1,0:T(8,128)(2,1)}, bf16[256,256]{1,0:T(8,128)(2,1)S(1)}, u32[]{:S(2)}, u32[]{:S(2)}) collective-permute-start(bf16[256,256]{1,0:T(8,128)(2,1)} %bitcast.11), channel_id=1, source_target_pairs={{0,16},{16,0},{1,17},{17,1},{2,18},{18,2},{3,19},{19,3},{4,20},{20... | collective-permute-start | bytes 393224 | tf_op jit(solution)/shard_map/ppermute | solution.py:227
  1.3 1.6 %copy-start.2 = (bf16[4096,128]{1,0:T(8,128)(2,1)S(1)}, bf16[4096,128]{1,0:T(8,128)(2,1)}, u32[]{:S(2)}) copy-start(bf16[4096,128]{1,0:T(8,128)(2,1)} %weight_k.1) | copy-start | bytes 3145732
  1.3 1.6 %copy-start.3 = (bf16[4096,128]{1,0:T(8,128)(2,1)S(1)}, bf16[4096,128]{1,0:T(8,128)(2,1)}, u32[]{:S(2)}) copy-start(bf16[4096,128]{1,0:T(8,128)(2,1)} %weight_v.1) | copy-start | bytes 3145732
  1.3 1.6 %copy-start.5 = (bf16[1,256,256]{2,1,0:T(8,128)(2,1)S(1)}, bf16[1,256,256]{2,1,0:T(8,128)(2,1)}, u32[]{:S(2)}) copy-start(bf16[1,256,256]{2,1,0:T(8,128)(2,1)} %param.13) | copy-start | bytes 393220
  1.3 1.6 %copy-start.6 = (bf16[1,256,256]{2,1,0:T(8,128)(2,1)S(1)}, bf16[1,256,256]{2,1,0:T(8,128)(2,1)}, u32[]{:S(2)}) copy-start(bf16[1,256,256]{2,1,0:T(8,128)(2,1)} %param.14) | copy-start | bytes 393220
  1.3 1.6 %copy-start.7 = (f32[32,128]{1,0:T(8,128)S(1)}, f32[32,128]{1,0:T(8,128)}, u32[]{:S(2)}) copy-start(f32[32,128]{1,0:T(8,128)} %position.1) | copy-start | bytes 49156
  1.3 1.6 %copy-start.9 = (bf16[1,4,1024]{2,1,0:T(4,128)(2,1)S(1)}, bf16[1,4,1024]{2,1,0:T(4,128)(2,1)}, u32[]{:S(2)}) copy-start(bf16[1,4,1024]{2,1,0:T(4,128)(2,1)} %param.12) | copy-start | bytes 24580
  1.3 2.8 %copy-start.4 = (bf16[4,8,2048]{2,1,0:T(8,128)(2,1)S(1)}, bf16[4,8,2048]{2,1,0:T(8,128)(2,1)}, u32[]{:S(2)}) copy-start(bf16[4,8,2048]{2,1,0:T(8,128)(2,1)} %residual.1) | copy-start | bytes 393220
  1.3 1.5 %collective-permute-start.2 = (bf16[4,1024]{1,0:T(4,128)(2,1)}, bf16[4,1024]{1,0:T(4,128)(2,1)S(1)}, u32[]{:S(2)}, u32[]{:S(2)}) collective-permute-start(bf16[4,1024]{1,0:T(4,128)(2,1)} %bitcast.16), channel_id=1, source_target_pairs={{0,16},{16,0},{1,17},{17,1},{2,18},{18,2},{3,19},{19,3},{4,20},{20... | collective-permute-start | bytes 24584 | tf_op jit(solution)/shard_map/ppermute | solution.py:227
  1.8 2.6 %copy-start = (bf16[1024,2048]{1,0:T(8,128)(2,1)S(1)}, bf16[1024,2048]{1,0:T(8,128)(2,1)}, u32[]{:S(2)}) copy-start(bf16[1024,2048]{1,0:T(8,128)(2,1)} %out_proj.1) | copy-start | bytes 12582916
  1.8 13.9 %copy-start.11 = (s32[4]{0:T(128)S(1)}, s32[4]{0:T(128)}, u32[]{:S(2)}) copy-start(s32[4]{0:T(128)} %param.23) | copy-start | bytes 52
  1.8 14.0 %copy-start.10 = (s32[4,8]{1,0:T(4,128)S(1)}, s32[4,8]{1,0:T(4,128)}, u32[]{:S(2)}) copy-start(s32[4,8]{1,0:T(4,128)} %param.22) | copy-start | bytes 388
  1.8 22.9 %copy-start.1 = (bf16[256,4096]{1,0:T(8,128)(2,1)S(1)}, bf16[256,4096]{1,0:T(8,128)(2,1)}, u32[]{:S(2)}) copy-start(bf16[256,4096]{1,0:T(8,128)(2,1)} %refs_5_.1) | copy-start | bytes 6291460
  1.9 22.9 %copy-start.8 = (f32[4096]{0:T(1024)S(1)}, f32[4096]{0:T(1024)}, u32[]{:S(2)}) copy-start(f32[4096]{0:T(1024)} %param.20) | copy-start | bytes 49156
  5.1 4.3 %collective-permute-start.3 = (f32[8,2048]{1,0:T(8,128)S(1)}, f32[8,2048]{1,0:T(8,128)S(1)}, u32[]{:S(2)}, u32[]{:S(2)}) collective-permute-start(f32[8,2048]{1,0:T(8,128)S(1)} %product.1), channel_id=1, source_target_pairs={{0,16},{16,0},{1,17},{17,1},{2,18},{18,2},{3,19},{19,3},{4,20},{20... | collective-permute-start | bytes 196616 | tf_op jit(solution)/shard_map/ppermute | solution.py:227
  5.4 4.9 %collective-permute-start.4 = (f32[8,2048]{1,0:T(8,128)S(1)}, f32[8,2048]{1,0:T(8,128)S(1)}, u32[]{:S(2)}, u32[]{:S(2)}) collective-permute-start(f32[8,2048]{1,0:T(8,128)S(1)} %product.1), channel_id=1, source_target_pairs={{0,20},{4,16},{8,28},{12,24},{16,4},{20,0},{24,12},{28,8},{1,21},{... | collective-permute-start | bytes 196616 | tf_op jit(solution)/shard_map/ppermute | solution.py:237
  8.0 4.0 %collective-permute-start.5 = (f32[8,2048]{1,0:T(8,128)S(1)}, f32[8,2048]{1,0:T(8,128)S(1)}, u32[]{:S(2)}, u32[]{:S(2)}) collective-permute-start(f32[8,2048]{1,0:T(8,128)S(1)} %product.1), channel_id=1, source_target_pairs={{0,24},{4,28},{8,16},{12,20},{16,8},{20,12},{24,0},{28,4},{1,25},{... | collective-permute-start | bytes 196616 | tf_op jit(solution)/shard_map/ppermute | solution.py:237
  9.3 4.8 %collective-permute-start.6 = (f32[8,2048]{1,0:T(8,128)S(1)}, f32[8,2048]{1,0:T(8,128)S(1)}, u32[]{:S(2)}, u32[]{:S(2)}) collective-permute-start(f32[8,2048]{1,0:T(8,128)S(1)} %product.1), channel_id=1, source_target_pairs={{0,28},{4,24},{8,20},{12,16},{16,12},{20,8},{24,4},{28,0},{1,29},{... | collective-permute-start | bytes 196616 | tf_op jit(solution)/shard_map/ppermute | solution.py:237
  14.1 4.5 %collective-permute-start.8 = (bf16[8,2048]{1,0:T(8,128)(2,1)S(1)}, bf16[8,2048]{1,0:T(8,128)(2,1)S(1)}, u32[]{:S(2)}, u32[]{:S(2)}) collective-permute-start(bf16[8,2048]{1,0:T(8,128)(2,1)S(1)} %add_convert_fusion.refs_2_), channel_id=1, source_target_pairs={{0,17},{1,16},{2,19},{3,18},{16,1},{17,0},{18,3},{19,2},{4,21},{5,... | collective-permute-start | bytes 98312 | tf_op jit(solution)/shard_map/ppermute | solution.py:237
  15.9 5.1 %collective-permute-start.9 = (bf16[8,2048]{1,0:T(8,128)(2,1)S(1)}, bf16[8,2048]{1,0:T(8,128)(2,1)S(1)}, u32[]{:S(2)}, u32[]{:S(2)}) collective-permute-start(bf16[8,2048]{1,0:T(8,128)(2,1)S(1)} %add_convert_fusion.refs_2_), channel_id=1, source_target_pairs={{0,18},{1,19},{2,16},{3,17},{16,2},{17,3},{18,0},{19,1},{4,22},{5,... | collective-permute-start | bytes 98312 | tf_op jit(solution)/shard_map/ppermute | solution.py:237
  18.3 5.1 %collective-permute-start.10 = (bf16[8,2048]{1,0:T(8,128)(2,1)S(1)}, bf16[8,2048]{1,0:T(8,128)(2,1)S(1)}, u32[]{:S(2)}, u32[]{:S(2)}) collective-permute-start(bf16[8,2048]{1,0:T(8,128)(2,1)S(1)} %add_convert_fusion.refs_2_), channel_id=1, source_target_pairs={{0,19},{1,18},{2,17},{3,16},{16,3},{17,2},{18,1},{19,0},{4,23},{5,... | collective-permute-start | bytes 98312 | tf_op jit(solution)/shard_map/ppermute | solution.py:237
  18.5 5.3 %collective-permute-start.7 = (bf16[8,2048]{1,0:T(8,128)(2,1)S(1)}, bf16[8,2048]{1,0:T(8,128)(2,1)S(1)}, u32[]{:S(2)}, u32[]{:S(2)}) collective-permute-start(bf16[8,2048]{1,0:T(8,128)(2,1)S(1)} %add_convert_fusion.refs_2_), channel_id=1, source_target_pairs={{0,16},{16,0},{1,17},{17,1},{2,18},{18,2},{3,19},{19,3},{4,20},{20... | collective-permute-start | bytes 98312 | tf_op jit(solution)/shard_map/ppermute | solution.py:227
  23.4 1.3 %collective-permute-start.11 = (bf16[24,2048]{1,0:T(8,128)(2,1)S(1)}, bf16[24,2048]{1,0:T(8,128)(2,1)S(1)}, u32[]{:S(2)}, u32[]{:S(2)}) collective-permute-start(bf16[24,2048]{1,0:T(8,128)(2,1)S(1)} %constant_dynamic-update-slice_fusion.refs_1_), channel_id=1, source_target_pairs={{0,16},{16,0},{1,17},{17,1},{2,18},{18,2},{3,19},{19,3},{4,20},{20... | collective-permute-start | bytes 294920 | tf_op jit(solution)/shard_map/ppermute | solution.py:227
